TPU v7x, 32 devices: a whole 2x2x4 slice. The times are simulated.
32 devices in a mesh: dp: 8 (over z, x), mp: 4 (over y, core).
Axes of the slice: x: 2, y: 2, z: 4, core: 2. Of those that a mesh axis runs over, the one named last changes fastest.
Arguments:
- tokens_in: bfloat16 [12288, 768], P(('dp', 'mp')), may hold values from -6 to 6
- skip_tokens: bfloat16 [12288, 768], P(('dp', 'mp')), may hold values from -6 to 6
- caption_flag: int32 [32], P('dp'), may hold values 0 or 1
- caption_mask: int32 [32, 77], P('dp'), may hold values 0 or 1
- w_skip: bfloat16 [1536, 768], P('dp', 'mp'), may hold values from -0.15625 to 0.15625
- b_skip: float32 [768], P('mp'), may hold values from -1.5 to 1.5
- gain_attn: float32 [768], P('mp'), may hold values from 0.1 to 1.9
- shift_attn: float32 [768], P('mp'), may hold values from -1.5 to 1.5
- w_qkv: bfloat16 [768, 3, 768], P('dp', None, 'mp'), may hold values from -0.21875 to 0.21875
- b_qv: float32 [2, 768], P(None, 'mp'), may hold values from -1.5 to 1.5
- w_out: bfloat16 [768, 768], P('mp', 'dp'), may hold values from -0.875 to 0.875
- b_out: float32 [768], P('mp'), may hold values from -1.5 to 1.5
- gain_mlp: float32 [768], P('mp'), may hold values from 0.1 to 1.9
- shift_mlp: float32 [768], P('mp'), may hold values from -1.5 to 1.5
- w_up: bfloat16 [768, 3072], P('dp', 'mp'), may hold values from -0.21875 to 0.21875
- b_up: float32 [3072], P('mp'), may hold values from -1.5 to 1.5
- w_down: bfloat16 [3072, 768], P('mp', 'dp'), may hold values from -0.15625 to 0.15625
- b_down: float32 [768], P('mp'), may hold values from -1.5 to 1.5
- cotangent: bfloat16 [12288, 768], P(('dp', 'mp')), may hold values from -6 to 6
Outputs:
- layer_out: bfloat16 [12288, 768], P(('dp', 'mp'))
- grad_tokens: float32 [12288, 768], P(('dp', 'mp'))
- grad_skip: float32 [12288, 768], P(('dp', 'mp'))
- grad_w_skip: float32 [1536, 768], P('dp', 'mp')
- grad_b_skip: float32 [768], P('mp')
- grad_gain_attn: float32 [768], P('mp')
- grad_shift_attn: float32 [768], P('mp')
- grad_w_qkv: float32 [768, 3, 768], P('dp', None, 'mp')
- grad_b_qv: float32 [2, 768], P(None, 'mp')
- grad_w_out: float32 [768, 768], P('mp', 'dp')
- grad_b_out: float32 [768], P('mp')
- grad_gain_mlp: float32 [768], P('mp')
- grad_shift_mlp: float32 [768], P('mp')
- grad_w_up: float32 [768, 3072], P('dp', 'mp')
- grad_b_up: float32 [3072], P('mp')
- grad_w_down: float32 [3072, 768], P('mp', 'dp')
- grad_b_down: float32 [768], P('mp')
All inputs are finite; a program needn't handle non-finite values. No bound on the sum of `caption_flag` or of `caption_mask` on one device may be relied on, other than what follows from the above.
Results may differ from a plain program's by a relative error of at most 0.014.
Values may be sent and summed in bfloat16 or wider, within the bound.
A program may use at most 128 MiB of HBM per device.

v0:
```python
import math

import jax
import jax.numpy as jnp
from jax import lax
from jax.sharding import PartitionSpec as P

HEAD = 64
LAT = 257


norm_eps = 1e-05
inv_root_two = 0.7071067811865476
inv_root_tau = 0.3989422804014327


def contract_rows(first_matrix, second_matrix):
    return lax.dot_general(
        first_matrix, second_matrix, (((0,), (0,)), ((), ())), preferred_element_type=jnp.float32
    )


def contract_cols(first_matrix, second_matrix):
    return lax.dot_general(
        first_matrix, second_matrix, (((1,), (1,)), ((), ())), preferred_element_type=jnp.float32
    )


def pair_sums(first_terms, second_terms):
    return lax.psum((jnp.sum(first_terms, axis=1), jnp.sum(second_terms, axis=1)), "mp")


def whole_rows(piece):
    return lax.all_gather(piece, "mp", axis=1, tiled=True)


def norm_forward(hidden, norm_gain, norm_shift):
    full_width = hidden.shape[1] * lax.axis_size("mp")
    totals = pair_sums(hidden, hidden * hidden)
    row_mean = totals[0][:, None] / full_width
    row_var = totals[1][:, None] / full_width - row_mean * row_mean
    inverse = lax.rsqrt(row_var + norm_eps)
    centred = (hidden - row_mean) * inverse
    normed = (centred * norm_gain + norm_shift).astype(jnp.bfloat16)
    return (whole_rows(normed), centred, inverse)


def norm_backward(normed_grad, centred, inverse, norm_gain):
    full_width = normed_grad.shape[1] * lax.axis_size("mp")
    scaled = normed_grad * norm_gain
    totals = pair_sums(scaled, scaled * centred)
    hidden_grad = inverse * (
        scaled - totals[0][:, None] / full_width - centred * totals[1][:, None] / full_width
    )
    return (hidden_grad, jnp.sum(normed_grad * centred, axis=0), jnp.sum(normed_grad, axis=0))


def feature_total(partial_value):
    return lax.psum_scatter(partial_value, "mp", scatter_dimension=1, tiled=True)


def head_total(partial_value):
    return lax.psum_scatter(partial_value, "mp", scatter_dimension=1, tiled=True)


def local(
    tokens_in,
    skip_tokens,
    caption_flag,
    caption_mask,
    w_skip,
    b_skip,
    gain_attn,
    shift_attn,
    w_qkv,
    b_qv,
    w_out,
    b_out,
    gain_mlp,
    shift_mlp,
    w_up,
    b_up,
    w_down,
    b_down,
    cotangent,
):
    item_count = caption_flag.shape[0]
    row_count = tokens_in.shape[0] * lax.axis_size("mp")
    slot_rows = row_count // item_count
    caption_width = caption_mask.shape[1]
    heads_here = w_qkv.shape[2] // HEAD
    col_width = w_qkv.shape[2]
    score_scale = 1.0 / math.sqrt(HEAD)
    positions = jnp.arange(slot_rows, dtype=jnp.int32)
    padded = jnp.concatenate(
        [
            jnp.zeros((item_count, LAT), jnp.int32),
            caption_mask,
            jnp.zeros((item_count, slot_rows - LAT - caption_width), jnp.int32),
        ],
        axis=1,
    )
    live_mask = jnp.where(positions[None, :] < LAT, 1, caption_flag[:, None] * padded)
    key_keep = (live_mask > 0)[:, None, None, :]
    live_col = live_mask.reshape(row_count, 1).astype(jnp.float32)

    def heads_view(array):
        return array.reshape(item_count, slot_rows, heads_here, HEAD)

    def attention_probs(query_heads, key_heads, log_total):
        raw_scores = (
            jnp.einsum(
                "isha,itha->ihst", query_heads, key_heads, preferred_element_type=jnp.float32
            )
            * score_scale
        )
        masked = jnp.where(key_keep, raw_scores, -1e30)
        if log_total is None:
            top_score = jnp.max(masked, axis=-1, keepdims=True)
            log_total = top_score + jnp.log(
                jnp.sum(jnp.exp(masked - top_score), axis=-1, keepdims=True)
            )
        return (jnp.exp(masked - log_total), log_total)

    shards = (w_skip, w_qkv, w_up, w_out, w_down)
    skip_mat, qkv_mat, up_mat, out_mat, down_mat = (
        lax.all_gather(shards[0], "dp", axis=0, tiled=True),
        lax.all_gather(shards[1], "dp", axis=0, tiled=True),
        lax.all_gather(shards[2], "dp", axis=0, tiled=True),
        lax.all_gather(shards[3], "dp", axis=1, tiled=True),
        lax.all_gather(shards[4], "dp", axis=1, tiled=True),
    )
    tokens_all, skip_all, cotangent_all = (
        lax.all_gather(tokens_in, "mp", axis=0, tiled=True),
        lax.all_gather(skip_tokens, "mp", axis=0, tiled=True),
        lax.all_gather(cotangent, "mp", axis=0, tiled=True),
    )
    joined = jnp.concatenate([tokens_all, skip_all], axis=1)
    stream_zero = jnp.dot(joined, skip_mat, preferred_element_type=jnp.float32) + b_skip
    normed_one, centred_one, inverse_one = norm_forward(stream_zero, gain_attn, shift_attn)
    project = jnp.einsum("rd,dtc->rtc", normed_one, qkv_mat, preferred_element_type=jnp.float32)
    query_heads = heads_view((project[:, 0] + b_qv[0]).astype(jnp.bfloat16))
    key_heads = heads_view(project[:, 1].astype(jnp.bfloat16))
    value_heads = heads_view((project[:, 2] + b_qv[1]).astype(jnp.bfloat16))
    probs, log_total = attention_probs(query_heads, key_heads, None)
    context = (
        jnp.einsum(
            "ihst,itha->isha",
            probs.astype(jnp.bfloat16),
            value_heads,
            preferred_element_type=jnp.float32,
        )
        .astype(jnp.bfloat16)
        .reshape(row_count, -1)
    )
    attn_out = head_total(jnp.dot(context, out_mat, preferred_element_type=jnp.float32)) + b_out
    stream_one = stream_zero + attn_out
    normed_two, centred_two, inverse_two = norm_forward(stream_one, gain_mlp, shift_mlp)
    pre_act = jnp.dot(normed_two, up_mat, preferred_element_type=jnp.float32) + b_up
    hidden_low = jax.nn.gelu(pre_act, approximate=False).astype(jnp.bfloat16)
    mlp_out = (
        feature_total(jnp.dot(hidden_low, down_mat, preferred_element_type=jnp.float32)) + b_down
    )
    out_cols = ((stream_one + mlp_out) * live_col).astype(jnp.bfloat16)
    layer_out = lax.all_to_all(out_cols, "mp", split_axis=0, concat_axis=1, tiled=True)
    upstream_all = cotangent_all * live_col.astype(jnp.bfloat16)
    upstream = lax.dynamic_slice_in_dim(
        upstream_all, lax.axis_index("mp") * col_width, col_width, 1
    ).astype(jnp.float32)
    grad_b_down = jnp.sum(upstream, axis=0)
    grad_w_down = contract_rows(hidden_low, upstream_all)
    hidden_grad = contract_cols(upstream_all, down_mat)
    normal_cdf = 0.5 * (1.0 + lax.erf(pre_act * inv_root_two))
    normal_pdf = jnp.exp(-0.5 * pre_act * pre_act) * inv_root_tau
    pre_grad = (hidden_grad * (normal_cdf + pre_act * normal_pdf)).astype(jnp.bfloat16)
    grad_b_up = jnp.sum(pre_grad.astype(jnp.float32), axis=0)
    grad_w_up = contract_rows(normed_two, pre_grad)
    normed_grad_two = feature_total(contract_cols(pre_grad, up_mat))
    back_two, grad_gain_mlp, grad_shift_mlp = norm_backward(
        normed_grad_two, centred_two, inverse_two, gain_mlp
    )
    stream_grad = upstream + back_two
    attn_grad = stream_grad.astype(jnp.bfloat16)
    grad_b_out = jnp.sum(attn_grad.astype(jnp.float32), axis=0)
    attn_all = whole_rows(attn_grad)
    grad_w_out = contract_rows(context, attn_all)
    context_heads = heads_view(contract_cols(attn_all, out_mat).astype(jnp.bfloat16))
    probs_again, unused_total = attention_probs(query_heads, key_heads, log_total)
    probs_grad = jnp.einsum(
        "isha,itha->ihst", context_heads, value_heads, preferred_element_type=jnp.float32
    )
    row_dot = jnp.sum(probs_grad * probs_again, axis=-1, keepdims=True)
    score_grad = (probs_again * (probs_grad - row_dot)).astype(jnp.bfloat16)
    query_grad = (
        (
            jnp.einsum("ihst,itha->isha", score_grad, key_heads, preferred_element_type=jnp.float32)
            * score_scale
        )
        .astype(jnp.bfloat16)
        .reshape(row_count, -1)
    )
    key_grad = (
        (
            jnp.einsum(
                "ihst,isha->itha", score_grad, query_heads, preferred_element_type=jnp.float32
            )
            * score_scale
        )
        .astype(jnp.bfloat16)
        .reshape(row_count, -1)
    )
    value_grad = (
        jnp.einsum(
            "ihst,isha->itha",
            probs_again.astype(jnp.bfloat16),
            context_heads,
            preferred_element_type=jnp.float32,
        )
        .astype(jnp.bfloat16)
        .reshape(row_count, -1)
    )
    project_grad = jnp.stack([query_grad, key_grad, value_grad], axis=1)
    grad_b_qv = jnp.stack(
        [
            jnp.sum(query_grad.astype(jnp.float32), axis=0),
            jnp.sum(value_grad.astype(jnp.float32), axis=0),
        ],
        axis=0,
    )
    grad_w_qkv = jnp.einsum(
        "rd,rtc->dtc", normed_one, project_grad, preferred_element_type=jnp.float32
    )
    normed_grad_one = head_total(
        jnp.einsum("rtc,dtc->rd", project_grad, qkv_mat, preferred_element_type=jnp.float32)
    )
    back_one, grad_gain_attn, grad_shift_attn = norm_backward(
        normed_grad_one, centred_one, inverse_one, gain_attn
    )
    base_grad = (stream_grad + back_one).astype(jnp.bfloat16)
    grad_b_skip = jnp.sum(base_grad.astype(jnp.float32), axis=0)
    grad_w_skip = contract_rows(joined, base_grad)
    input_part = contract_cols(base_grad, skip_mat)
    input_grad = lax.psum_scatter(input_part, "mp", scatter_dimension=0, tiled=True)
    full_width = input_grad.shape[1] // 2
    big_grads = (
        lax.psum_scatter(grad_w_skip, "dp", scatter_dimension=0, tiled=True),
        lax.psum_scatter(grad_w_qkv, "dp", scatter_dimension=0, tiled=True),
        lax.psum_scatter(grad_w_up, "dp", scatter_dimension=0, tiled=True),
        lax.psum_scatter(grad_w_out, "dp", scatter_dimension=1, tiled=True),
        lax.psum_scatter(grad_w_down, "dp", scatter_dimension=1, tiled=True),
    )
    small_grads = lax.psum(
        (
            grad_b_skip,
            grad_gain_attn,
            grad_shift_attn,
            grad_b_qv,
            grad_b_out,
            grad_gain_mlp,
            grad_shift_mlp,
            grad_b_up,
            grad_b_down,
        ),
        "dp",
    )
    return (
        layer_out,
        input_grad[:, :full_width],
        input_grad[:, full_width:],
        big_grads[0],
        small_grads[0],
        small_grads[1],
        small_grads[2],
        big_grads[1],
        small_grads[3],
        big_grads[3],
        small_grads[4],
        small_grads[5],
        small_grads[6],
        big_grads[2],
        small_grads[7],
        big_grads[4],
        small_grads[8],
    )


def solution(mesh):
    in_specs = (
        P(("dp", "mp"), None),
        P(("dp", "mp"), None),
        P("dp"),
        P("dp", None),
        P("dp", "mp"),
        P("mp"),
        P("mp"),
        P("mp"),
        P("dp", None, "mp"),
        P(None, "mp"),
        P("mp", "dp"),
        P("mp"),
        P("mp"),
        P("mp"),
        P("dp", "mp"),
        P("mp"),
        P("mp", "dp"),
        P("mp"),
        P(("dp", "mp"), None),
    )
    out_specs = (
        P(("dp", "mp"), None),
        P(("dp", "mp"), None),
        P(("dp", "mp"), None),
        P("dp", "mp"),
        P("mp"),
        P("mp"),
        P("mp"),
        P("dp", None, "mp"),
        P(None, "mp"),
        P("mp", "dp"),
        P("mp"),
        P("mp"),
        P("mp"),
        P("dp", "mp"),
        P("mp"),
        P("mp", "dp"),
        P("mp"),
    )
    return jax.shard_map(local, mesh=mesh, in_specs=in_specs, out_specs=out_specs, check_vma=False)
```

profile of v0, /device:TPU:0, one launch (start us, length us, event | category | flops | bytes accessed | tf_op | source)
XLA Modules:
  0.0 1024.7 jit_solution(11836900614168077589)
XLA Ops:
  8.7 34.1 %all_gather.35 = bf16[1536,192]{1,0:T(8,128)(2,1)S(1)} all-gather(bf16[192,192]{1,0:T(8,128)(2,1)} %param.23), channel_id=1, replica_groups=mesh['dp'=8,'mp'=4] {'dp'}, dimensions={0}, use_global_device_ids=true | all-gather | bytes 663552 | tf_op jit(solution)/shard_map/all_gather | solution.py:127
  46.6 15.4 %all-gather.11.cloned.1.call-done = bf16[1536,768]{1,0:T(8,128)(2,1)} async-done(((bf16[384,768]{1,0:T(8,128)(2,1)}), bf16[1536,768]{1,0:T(8,128)(2,1)}) %all-gather.11.cloned.1.call-update) | async-done | bytes 2359312 | tf_op jit(solution)/shard_map/all_gather | solution.py:135
  69.4 10.4 %all-reduce.4 = (f32[1536]{0:T(1024)S(1)}, f32[1536]{0:T(1024)S(1)}) all-reduce(f32[1536]{0:T(1024)S(1)} %get-tuple-element.62, f32[1536]{0:T(1024)S(1)} %get-tuple-element.61), channel_id=1, replica_groups=mesh['dp'=8,'mp'=4] {'mp'}, use_global_device_ids=true, to_apply=%region_3.4 | all-reduce | flops 3072 | bytes 24576 | tf_op jit(solution)/shard_map/psum | solution.py:30
  82.1 37.7 %all_gather.37 = bf16[768,3,192]{2,1,0:T(4,128)(2,1)S(1)} all-gather(bf16[96,3,192]{2,1,0:T(4,128)(2,1)S(1)} %copy.69), channel_id=1, replica_groups=mesh['dp'=8,'mp'=4] {'dp'}, dimensions={0}, use_global_device_ids=true | all-gather | bytes 995328 | tf_op jit(solution)/shard_map/all_gather | solution.py:128
  122.0 31.2 %all_gather.38 = bf16[192,768]{0,1:T(8,128)(2,1)S(1)} all-gather(bf16[192,96]{0,1:T(8,128)(2,1)S(1)} %copy.76), channel_id=1, replica_groups=mesh['dp'=8,'mp'=4] {'dp'}, dimensions={1}, use_global_device_ids=true | all-gather | bytes 331776 | tf_op jit(solution)/shard_map/all_gather | solution.py:130
  176.3 44.6 %reduce-scatter.13.cloned.1.call-done = f32[1536,192]{0,1:T(8,128)} async-done(((f32[1536,768]{0,1:T(8,128)}), f32[1536,192]{0,1:T(8,128)}) %reduce-scatter.13.cloned.1.call-update) | async-done | bytes 1179664 | tf_op jit(solution)/shard_map/reduce_scatter | solution.py:63
  222.5 10.4 %all-reduce.3 = (f32[1536]{0:T(1024)S(1)}, f32[1536]{0:T(1024)S(1)}) all-reduce(f32[1536]{0:T(1024)S(1)} %get-tuple-element.60, f32[1536]{0:T(1024)S(1)} %get-tuple-element.59), channel_id=1, replica_groups=mesh['dp'=8,'mp'=4] {'mp'}, use_global_device_ids=true, to_apply=%region_10.11 | all-reduce | flops 3072 | bytes 24576 | tf_op jit(solution)/shard_map/psum | solution.py:30
  235.0 11.5 %all-gather.21.cloned.1.call-done = bf16[1536,768]{0,1:T(8,128)(2,1)} async-done(((bf16[384,768]{0,1:T(8,128)(2,1)}), bf16[1536,768]{0,1:T(8,128)(2,1)}) %all-gather.21.cloned.1.call-update) | async-done | bytes 2359312 | tf_op jit(solution)/shard_map/all_gather | solution.py:136
  249.7 39.9 %all-gather.17.cloned.1.call-done = bf16[768,768]{1,0:T(8,128)(2,1)} async-done(((bf16[96,768]{1,0:T(8,128)(2,1)}), bf16[768,768]{1,0:T(8,128)(2,1)}) %all-gather.17.cloned.1.call-update) | async-done | bytes 1179664 | tf_op jit(solution)/shard_map/all_gather | solution.py:129
  289.6 24.9 %all-gather.15.cloned.1.call-done = bf16[1536,768]{0,1:T(8,128)(2,1)} async-done(((bf16[1536,192]{0,1:T(8,128)(2,1)}), bf16[1536,768]{0,1:T(8,128)(2,1)}) %all-gather.15.cloned.1.call-update) | async-done | bytes 2359312 | tf_op jit(solution)/shard_map/all_gather | solution.py:34
  314.5 14.9 %fusion.3 = (bf16[1536,768]{1,0:T(8,128)(2,1)}, f32[1536,768]{1,0:T(8,128)}) fusion(f32[768]{0:T(1024)S(1)} %copy-done.55, bf16[1536,768]{0,1:T(8,128)(2,1)} %all-gather.15.cloned.1.call-done, bf16[768,768]{1,0:T(8,128)(2,1)} %all-gather.17.cloned.1.call-done), kind=kOutput, calls=%fused_computation.10 | convolution fusion | flops 1889796096 | bytes 10619904 | tf_op jit(solution)/shard_map/dot_general | solution.py:159
  329.4 28.5 %all-gather.19.cloned.1.call-done = bf16[768,768]{0,1:T(8,128)(2,1)} async-done(((bf16[768,96]{0,1:T(8,128)(2,1)}), bf16[768,768]{0,1:T(8,128)(2,1)}) %all-gather.19.cloned.1.call-update) | async-done | bytes 1179664 | tf_op jit(solution)/shard_map/all_gather | solution.py:131
  357.9 6.7 convert_reduce_fusion
  370.2 46.8 %reduce-scatter.17.cloned.1.call-done = f32[1536,192]{0,1:T(8,128)} async-done(((f32[1536,768]{0,1:T(8,128)}), f32[1536,192]{0,1:T(8,128)}) %reduce-scatter.17.cloned.1.call-update) | async-done | bytes 1179664 | tf_op jit(solution)/shard_map/reduce_scatter | solution.py:59
  419.4 10.1 all-reduce.2
  432.9 24.5 %all-gather.23.cloned.1.call-done = bf16[1536,768]{0,1:T(8,128)(2,1)} async-done(((bf16[1536,192]{0,1:T(8,128)(2,1)}), bf16[1536,768]{0,1:T(8,128)(2,1)}) %all-gather.23.cloned.1.call-update) | async-done | bytes 2359312 | tf_op jit(solution)/shard_map/all_gather | solution.py:34
  463.1 5.8 convert_reduce_fusion.3
  496.0 36.5 %reduce-scatter.19.cloned.1.call-done = f32[1536,192]{0,1:T(8,128)} async-done(((f32[1536,768]{0,1:T(8,128)}), f32[1536,192]{0,1:T(8,128)}) %reduce-scatter.19.cloned.1.call-update) | async-done | bytes 1179664 | tf_op jit(solution)/shard_map/reduce_scatter | solution.py:63
  534.9 11.3 %all-reduce.1 = (f32[1536]{0:T(1024)}, f32[1536]{0:T(1024)}) all-reduce(f32[1536]{0:T(1024)} %get-tuple-element.54, f32[1536]{0:T(1024)} %get-tuple-element.55), channel_id=1, replica_groups=mesh['dp'=8,'mp'=4] {'mp'}, use_global_device_ids=true, to_apply=%region_22.23 | all-reduce | flops 3072 | bytes 24576 | tf_op jit(solution)/shard_map/psum | solution.py:30
  547.5 35.4 %reduce-scatter.15.cloned.1.call-done = f32[1536,192]{0,1:T(8,128)} async-done(((f32[1536,768]{0,1:T(8,128)}), f32[1536,192]{0,1:T(8,128)}) %reduce-scatter.15.cloned.1.call-update) | async-done | bytes 1179664 | tf_op jit(solution)/shard_map/reduce_scatter | solution.py:59
  588.2 5.1 fusion.55
  595.1 5.1 fusion.57
  601.8 5.1 fusion.60
  608.4 5.1 fusion.18
  614.6 5.0 fusion.56
  624.2 25.8 %reduce-scatter.31.cloned.1.call-done = f32[96,192]{1,0:T(8,128)} async-done(((f32[768,192]{1,0:T(8,128)}), f32[96,192]{1,0:T(8,128)}) %reduce-scatter.31.cloned.1.call-update) | async-done | bytes 73744
  651.7 35.6 %all-reduce = (f32[192]{0:T(256)}, f32[192]{0:T(256)}, f32[192]{0:T(256)}, f32[2,192]{1,0:T(2,128)}, f32[192]{0:T(256)}, /*index=5*/f32[192]{0:T(256)}, f32[192]{0:T(256)}, f32[768]{0:T(1024)}, f32[192]{0:T(256)}) all-reduce(f32[192]{0:T(256)S(1)} %copy-done.43, f32[192]{0:T(256)S(1)} %copy-done.40, ...), channel_id=1, replica_groups=mesh['dp'=8,'mp'=4] {'dp'}, use_global_device_ids=true, to_apply=%region_26.27 | all-reduce | flops 2496 | bytes 19968 | tf_op jit(solution)/shard_map/psum | solution.py:252
  688.4 41.1 %reduce-scatter.21.cloned.1.call-done = f32[384,1536]{1,0:T(8,128)} async-done(((f32[1536,1536]{1,0:T(8,128)}), f32[384,1536]{1,0:T(8,128)}) %reduce-scatter.21.cloned.1.call-update) | async-done | bytes 2359312 | tf_op jit(solution)/shard_map/reduce_scatter | solution.py:243
  732.7 70.5 %reduce-scatter.27.cloned.1.call-done = f32[96,768]{1,0:T(8,128)} async-done(((f32[768,768]{1,0:T(8,128)}), f32[96,768]{1,0:T(8,128)}) %reduce-scatter.27.cloned.1.call-update) | async-done | bytes 294928 | tf_op jit(solution)/shard_map/reduce_scatter | solution.py:248
  803.2 72.7 %reduce-scatter.29.cloned.1.call-done = f32[768,96]{0,1:T(8,128)} async-done(((f32[768,768]{0,1:T(8,128)}), f32[768,96]{0,1:T(8,128)}) %reduce-scatter.29.cloned.1.call-update) | async-done | bytes 294928 | tf_op jit(solution)/shard_map/reduce_scatter | solution.py:250
  875.9 72.9 %reduce-scatter.25.cloned.1.call-done = f32[96,3,192]{2,0,1:T(8,128)} async-done(((f32[768,3,192]{2,0,1:T(8,128)}), f32[96,3,192]{2,0,1:T(8,128)}) %reduce-scatter.25.cloned.1.call-update) | async-done | bytes 221200 | tf_op jit(solution)/shard_map/reduce_scatter | solution.py:247
  948.8 68.7 %reduce-scatter.23.cloned.1.call-done = f32[192,192]{1,0:T(8,128)} async-done(((f32[1536,192]{1,0:T(8,128)}), f32[192,192]{1,0:T(8,128)}) %reduce-scatter.23.cloned.1.call-update) | async-done | bytes 147472 | tf_op jit(solution)/shard_map/reduce_scatter | solution.py:246
  (233 shorter events, 116.0 us)
Async XLA Ops:
  7.2 35.6 %all-gather.9.cloned.1.call-start = ((), (), s32[]{:S(2)}) async-start(), calls=%async_computation.11 | async-start | bytes 2949120 | tf_op jit(solution)/shard_map/all_gather | solution.py:134
  7.9 54.1 %all-gather.11.cloned.1.call-start = ((), (), s32[]{:S(2)}) async-start(), calls=%async_computation.12 | async-start | bytes 2949120 | tf_op jit(solution)/shard_map/all_gather | solution.py:135
  8.7 144.6 %all-gather.13.cloned.1.call-start = ((), (), s32[]{:S(2)}) async-start(), calls=%async_computation.13 | async-start | bytes 2949120 | tf_op jit(solution)/shard_map/all_gather | solution.py:34
  69.4 151.6 %copy-start.3 = (f32[1536,192]{0,1:T(8,128)}, f32[1536,192]{0,1:T(8,128)S(1)}, u32[]{:S(2)}) copy-start(f32[1536,192]{0,1:T(8,128)S(1)} %get-tuple-element.97) | copy-start | bytes 3538948
  81.5 139.4 %reduce-scatter.13.cloned.1.call-start = ((), (), s32[]{:S(2)}) async-start(), calls=%async_computation.14 | async-start | bytes 5898240 | tf_op jit(solution)/shard_map/reduce_scatter | solution.py:63
  81.8 85.0 %copy-start.32 = (f32[3,64]{1,0:T(4,128)}, f32[3,64]{1,0:T(4,128)S(1)}, u32[]{:S(2)}) copy-start(f32[3,64]{1,0:T(4,128)S(1)} %add.166) | copy-start | bytes 2308
  82.1 71.1 %copy-start.36 = (s32[4,77]{1,0:T(4,128)S(1)}, s32[4,77]{1,0:T(4,128)}, u32[]{:S(2)}) copy-start(s32[4,77]{1,0:T(4,128)} %param.22) | copy-start | bytes 3700
  82.1 71.1 %copy-start.48 = (s32[4]{0:T(128)S(1)}, s32[4]{0:T(128)}, u32[]{:S(2)}) copy-start(s32[4]{0:T(128)} %param.21) | copy-start | bytes 52
  173.5 47.5 %copy-start.51 = (f32[192]{0:T(256)S(1)}, f32[192]{0:T(256)}, u32[]{:S(2)}) copy-start(f32[192]{0:T(256)} %param.30) | copy-start | bytes 2308
  173.5 72.9 %all-gather.21.cloned.1.call-start = ((), (), s32[]{:S(2)}) async-start(), calls=%async_computation.19 | async-start | bytes 2949120 | tf_op jit(solution)/shard_map/all_gather | solution.py:136
  175.6 57.3 %copy-start.34 = (f32[192]{0:T(256)S(1)}, f32[192]{0:T(256)}, u32[]{:S(2)}) copy-start(f32[192]{0:T(256)} %param.31) | copy-start | bytes 2308
  175.6 57.3 %copy-start.50 = (f32[192]{0:T(256)S(1)}, f32[192]{0:T(256)}, u32[]{:S(2)}) copy-start(f32[192]{0:T(256)} %param.32) | copy-start | bytes 2308
  175.6 113.9 %all-gather.17.cloned.1.call-start = ((), (), s32[]{:S(2)}) async-start(), calls=%async_computation.16 | async-start | bytes 1327104 | tf_op jit(solution)/shard_map/all_gather | solution.py:129
  176.2 138.3 %all-gather.15.cloned.1.call-start = ((), (), s32[]{:S(2)}) async-start(), calls=%async_computation.15 | async-start | bytes 2949120 | tf_op jit(solution)/shard_map/all_gather | solution.py:34
  222.5 207.1 %copy-start.1 = (f32[1536,192]{0,1:T(8,128)}, f32[1536,192]{0,1:T(8,128)S(1)}, u32[]{:S(2)}) copy-start(f32[1536,192]{0,1:T(8,128)S(1)} %get-tuple-element.86) | copy-start | bytes 3538948
  234.0 123.8 %all-gather.19.cloned.1.call-start = ((), (), s32[]{:S(2)}) async-start(), calls=%async_computation.17 | async-start | bytes 1327104 | tf_op jit(solution)/shard_map/all_gather | solution.py:131
  234.8 182.2 %reduce-scatter.17.cloned.1.call-start = ((), (), s32[]{:S(2)}) async-start(), calls=%async_computation.20 | async-start | bytes 5898240 | tf_op jit(solution)/shard_map/reduce_scatter | solution.py:59
  234.9 79.6 %copy-start.55 = (f32[768]{0:T(1024)S(1)}, f32[768]{0:T(1024)}, u32[]{:S(2)}) copy-start(f32[768]{0:T(1024)} %param.34) | copy-start | bytes 9220
  370.2 87.2 %all-gather.23.cloned.1.call-start = ((), (), s32[]{:S(2)}) async-start(), calls=%async_computation.21 | async-start | bytes 2949120 | tf_op jit(solution)/shard_map/all_gather | solution.py:34
  432.6 99.9 %reduce-scatter.19.cloned.1.call-start = ((), (), s32[]{:S(2)}) async-start(), calls=%async_computation.22 | async-start | bytes 5898240 | tf_op jit(solution)/shard_map/reduce_scatter | solution.py:63
  484.4 98.5 %reduce-scatter.15.cloned.1.call-start = ((), (), s32[]{:S(2)}) async-start(), calls=%async_computation.18 | async-start | bytes 5898240 | tf_op jit(solution)/shard_map/reduce_scatter | solution.py:59
  490.8 41.7 %copy-start.4 = (f32[1536,192]{0,1:T(8,128)S(1)}, f32[1536,192]{0,1:T(8,128)}, u32[]{:S(2)}) copy-start(f32[1536,192]{0,1:T(8,128)} %copy-done.3) | copy-start | bytes 3538948
  490.8 159.2 %reduce-scatter.31.cloned.1.call-start = ((), (), s32[]{:S(2)}) async-start(), calls=%async_computation.28 | async-start | bytes 884736
  495.9 87.0 %copy-start.2 = (f32[1536,192]{0,1:T(8,128)S(1)}, f32[1536,192]{0,1:T(8,128)}, u32[]{:S(2)}) copy-start(f32[1536,192]{0,1:T(8,128)} %copy-done.1) | copy-start | bytes 3538948
  495.9 87.0 %copy-start.8 = (f32[1536,192]{0,1:T(8,128)S(1)}, f32[1536,192]{0,1:T(8,128)}, u32[]{:S(2)}) copy-start(f32[1536,192]{0,1:T(8,128)} %reduce-scatter.17.cloned.1.call-done) | copy-start | bytes 3538948
  495.9 233.6 %reduce-scatter.21.cloned.1.call-start = ((), (), s32[]{:S(2)}) async-start(), calls=%async_computation.23 | async-start | bytes 11796480 | tf_op jit(solution)/shard_map/reduce_scatter | solution.py:243
  593.4 209.8 %reduce-scatter.27.cloned.1.call-start = ((), (), s32[]{:S(2)}) async-start(), calls=%async_computation.26 | async-start | bytes 2654208 | tf_op jit(solution)/shard_map/reduce_scatter | solution.py:248
  600.1 275.7 %reduce-scatter.29.cloned.1.call-start = ((), (), s32[]{:S(2)}) async-start(), calls=%async_computation.27 | async-start | bytes 2654208 | tf_op jit(solution)/shard_map/reduce_scatter | solution.py:250
  606.9 341.8 %reduce-scatter.25.cloned.1.call-start = ((), (), s32[]{:S(2)}) async-start(), calls=%async_computation.25 | async-start | bytes 2654208 | tf_op jit(solution)/shard_map/reduce_scatter | solution.py:247
  613.6 403.9 %reduce-scatter.23.cloned.1.call-start = ((), (), s32[]{:S(2)}) async-start(), calls=%async_computation.24 | async-start | bytes 1769472 | tf_op jit(solution)/shard_map/reduce_scatter | solution.py:246
  619.6 32.1 %copy-start.39 = (f32[192]{0:T(256)S(1)}, f32[192]{0:T(256)}, u32[]{:S(2)}) copy-start(f32[192]{0:T(256)} %get-tuple-element.57) | copy-start | bytes 2308
  620.6 66.8 %all-to-all-start = ((bf16[4,384,192]{1,2,0:T(8,128)(2,1)}), bf16[4,384,192]{1,2,0:T(8,128)(2,1)S(1)}, u32[]{:S(2)}, u32[]{:S(2)}) async-start(bf16[4,384,192]{1,2,0:T(8,128)(2,1)} %bitcast.74), calls=%async_computation.2 | async-start | bytes 1179648 | tf_op jit(solution)/shard_map/all_to_all | solution.py:165
  (48 other events, 537.2 us)
Sparse Core Ops, SparseCore 0:
  9.6 26.7 all-gather.8
  37.9 24.0 all-gather.10
  81.6 25.0 all-gather.12
  173.6 47.2 reduce-scatter.12
  222.3 24.0 all-gather.20
  248.4 41.1 all-gather.16
  291.7 22.7 all-gather.14
  316.7 41.1 all-gather.18
  370.3 46.6 reduce-scatter.16
  432.7 24.6 all-gather.22
  484.5 47.9 reduce-scatter.18
  534.9 47.9 reduce-scatter.14
  586.8 63.2 reduce-scatter.30
  652.5 77.0 reduce-scatter.20
  733.4 69.6 reduce-scatter.26
  807.1 68.7 reduce-scatter.28
  879.8 68.9 reduce-scatter.24
  952.6 64.7 reduce-scatter.22
where the time goes:
time: 1030 us; the launch traced here: 1020 us
  waiting for transfers between devices  663 us (64%)
  blocking collectives  181 us (18%)
  matrix products  92.7 us (9%)
  local copies, waits for them, and re-layouts  44 us (4%)
  other arithmetic  24.6 us (2%)
  between operations  15.4 us (1%)
    reduce_scatter x2, waiting for transfers between devices, feature_total(): lax.psum_scatter(partial_value, 'mp', scatter_dimension=1, tiled=True)  82.2 us
    reduce_scatter x2, waiting for transfers between devices, head_total(): lax.psum_scatter(partial_value, 'mp', scatter_dimension=1, tiled=True)  81.2 us
    reduce_scatter x1, waiting for transfers between devices, local(): lax.psum_scatter(grad_w_qkv, 'dp', scatter_dimension=0, tiled=True)  72.9 us
    reduce_scatter x1, waiting for transfers between devices, local(): lax.psum_scatter(grad_w_down, 'dp', scatter_dimension=1, tiled=True)  72.7 us
    reduce_scatter x1, waiting for transfers between devices, local(): lax.psum_scatter(grad_w_up, 'dp', scatter_dimension=0, tiled=True)  70.5 us
    reduce_scatter x1, waiting for transfers between devices, local(): lax.psum_scatter(grad_w_skip, 'dp', scatter_dimension=0, tiled=True)  68.7 us
    all_gather x3, waiting for transfers between devices, whole_rows(): return lax.all_gather(piece, 'mp', axis=1, tiled=True)  49.4 us
    psum x4, blocking collectives, pair_sums(): lax.psum((jnp.sum(first_terms, axis=1), jnp.sum(second_terms, axis=1)), '...  42.2 us
  transfers between devices with their start and end apart: 19, of which 16 were waited for; matrix products, arithmetic and copies ran while one was open for 8% of the time, Pallas kernels for 0%

commit v1 on v0

v1 whole, which is shorter than its diff:
```python
import math

import jax
import jax.numpy as jnp
from jax import lax
from jax.sharding import PartitionSpec as P

HEAD = 64
LAT = 257
BF = jnp.bfloat16
F32 = jnp.float32

norm_eps = 1e-05
inv_root_two = 0.7071067811865476
inv_root_tau = 0.3989422804014327


def rows_t(a, b):
    return lax.dot_general(a, b, (((0,), (0,)), ((), ())), preferred_element_type=F32)


def cols_t(a, b):
    return lax.dot_general(a, b, (((1,), (1,)), ((), ())), preferred_element_type=F32)


def mm(a, b):
    return jnp.dot(a, b, preferred_element_type=F32)


def norm_forward(hidden, gain, shift):
    mean = jnp.mean(hidden, axis=1, keepdims=True)
    var = jnp.mean(hidden * hidden, axis=1, keepdims=True) - mean * mean
    inverse = lax.rsqrt(var + norm_eps)
    centred = (hidden - mean) * inverse
    return (centred * gain + shift).astype(BF), centred, inverse


def norm_backward(grad, centred, inverse, gain):
    scaled = grad * gain
    first = jnp.mean(scaled, axis=1, keepdims=True)
    second = jnp.mean(scaled * centred, axis=1, keepdims=True)
    out = inverse * (scaled - first - centred * second)
    return out, jnp.sum(grad * centred, axis=0), jnp.sum(grad, axis=0)


def item_compute(tokens, skip, cot, live, weights, small):
    w_skip, w_qkv, w_out_t, w_up, w_down_t = weights
    (b_skip, gain_attn, shift_attn, b_q, b_v, b_out, gain_mlp, shift_mlp, b_down, b_up) = small
    items, slot = live.shape
    rows, width = tokens.shape
    heads = width // HEAD
    scale = 1.0 / math.sqrt(HEAD)
    keep = (live > 0)[:, None, None, :]
    live_col = live.reshape(rows, 1).astype(F32)

    def split(a):
        return a.reshape(items, slot, heads, HEAD)

    joined = jnp.concatenate([tokens, skip], axis=1)
    h0 = mm(joined, w_skip) + b_skip
    n1, xhat1, inv1 = norm_forward(h0, gain_attn, shift_attn)
    q = split((mm(n1, w_qkv[0]) + b_q).astype(BF))
    k = split(mm(n1, w_qkv[1]).astype(BF))
    v = split((mm(n1, w_qkv[2]) + b_v).astype(BF))
    scores = jnp.einsum("isha,itha->ihst", q, k, preferred_element_type=F32) * scale
    scores = jnp.where(keep, scores, -1e30)
    top = jnp.max(scores, axis=-1, keepdims=True)
    weight = jnp.exp(scores - top)
    probs = weight / jnp.sum(weight, axis=-1, keepdims=True)
    probs_low = probs.astype(BF)
    ctx = jnp.einsum("ihst,itha->isha", probs_low, v, preferred_element_type=F32)
    ctx = ctx.astype(BF).reshape(rows, width)
    h1 = h0 + cols_t(ctx, w_out_t) + b_out
    n2, xhat2, inv2 = norm_forward(h1, gain_mlp, shift_mlp)
    pre = mm(n2, w_up) + b_up
    cdf = 0.5 * (1.0 + lax.erf(pre * inv_root_two))
    pdf = jnp.exp(-0.5 * pre * pre) * inv_root_tau
    hid = (pre * cdf).astype(BF)
    h2 = h1 + cols_t(hid, w_down_t) + b_down
    layer_out = (h2 * live_col).astype(BF)

    dy_low = cot * live_col.astype(BF)
    dy = dy_low.astype(F32)
    g_b_down = jnp.sum(dy, axis=0)
    g_w_down_t = rows_t(dy_low, hid)
    dhid = mm(dy_low, w_down_t)
    dpre = (dhid * (cdf + pre * pdf)).astype(BF)
    g_b_up = jnp.sum(dpre.astype(F32), axis=0)
    g_w_up = rows_t(n2, dpre)
    dn2 = cols_t(dpre, w_up)
    back2, g_gain_mlp, g_shift_mlp = norm_backward(dn2, xhat2, inv2, gain_mlp)
    dh1 = dy + back2
    dattn = dh1.astype(BF)
    g_b_out = jnp.sum(dattn.astype(F32), axis=0)
    g_w_out_t = rows_t(dattn, ctx)
    dctx = split(mm(dattn, w_out_t).astype(BF))
    dprobs = jnp.einsum("isha,itha->ihst", dctx, v, preferred_element_type=F32)
    dot = jnp.sum(dprobs * probs, axis=-1, keepdims=True)
    dscore = (probs * (dprobs - dot)).astype(BF)
    dq = (jnp.einsum("ihst,itha->isha", dscore, k, preferred_element_type=F32) * scale).astype(BF)
    dk = (jnp.einsum("ihst,isha->itha", dscore, q, preferred_element_type=F32) * scale).astype(BF)
    dv = jnp.einsum("ihst,isha->itha", probs_low, dctx, preferred_element_type=F32).astype(BF)
    dq, dk, dv = (a.reshape(rows, width) for a in (dq, dk, dv))
    g_b_q = jnp.sum(dq.astype(F32), axis=0)
    g_b_v = jnp.sum(dv.astype(F32), axis=0)
    g_w_qkv = (rows_t(n1, dq), rows_t(n1, dk), rows_t(n1, dv))
    dn1 = cols_t(dq, w_qkv[0]) + cols_t(dk, w_qkv[1]) + cols_t(dv, w_qkv[2])
    back1, g_gain_attn, g_shift_attn = norm_backward(dn1, xhat1, inv1, gain_attn)
    dh0 = (dh1 + back1).astype(BF)
    g_b_skip = jnp.sum(dh0.astype(F32), axis=0)
    g_w_skip = rows_t(joined, dh0)
    g_tokens = cols_t(dh0, w_skip[:width])
    g_skip = cols_t(dh0, w_skip[width:])
    return (
        layer_out,
        g_tokens,
        g_skip,
        (g_w_skip, g_w_qkv, g_w_out_t, g_w_up, g_w_down_t),
        (g_b_skip, g_gain_attn, g_shift_attn, g_b_q, g_b_v, g_b_out, g_gain_mlp, g_shift_mlp, g_b_down, g_b_up),
    )


def live_rows(caption_flag, caption_mask, slot):
    items, width = caption_mask.shape
    positions = jnp.arange(slot, dtype=jnp.int32)
    padded = jnp.concatenate(
        [
            jnp.zeros((items, LAT), jnp.int32),
            caption_mask,
            jnp.zeros((items, slot - LAT - width), jnp.int32),
        ],
        axis=1,
    )
    return jnp.where(positions[None, :] < LAT, 1, caption_flag[:, None] * padded)


def local(
    tokens_in,
    skip_tokens,
    caption_flag,
    caption_mask,
    w_skip,
    b_skip,
    gain_attn,
    shift_attn,
    w_qkv,
    b_qv,
    w_out,
    b_out,
    gain_mlp,
    shift_mlp,
    w_up,
    b_up,
    w_down,
    b_down,
    cotangent,
):
    n_dp, n_mp = lax.axis_size("dp"), lax.axis_size("mp")
    both = ("dp", "mp")
    column = lax.axis_index("mp")
    cols = b_skip.shape[0]
    items = caption_flag.shape[0] // n_mp
    slot = tokens_in.shape[0] // items
    live = live_rows(caption_flag, caption_mask, slot)
    live = lax.dynamic_slice_in_dim(live, column * items, items, 0)

    packed = jnp.stack(
        [b_skip, gain_attn, shift_attn, b_qv[0], b_qv[1], b_out, gain_mlp, shift_mlp, b_down]
        + [b_up.reshape(4, -1)[i] for i in range(4)]
    )
    packed = lax.all_gather(packed, "mp", axis=0)
    whole = packed[:, :9].transpose(1, 0, 2).reshape(9, -1)
    small = tuple(whole[i] for i in range(9)) + (packed[:, 9:].reshape(-1),)

    tiles = (w_skip, w_qkv.transpose(1, 0, 2), w_out.T, w_up, w_down.T)
    flat = jnp.concatenate([t.reshape(-1, 384) for t in tiles], axis=0)
    gathered = lax.all_gather(flat, both, axis=0)
    parts = []
    at = 0
    for t in tiles:
        count = t.size // 384
        part = gathered[:, at : at + count].reshape((n_dp, n_mp) + t.shape)
        at += count
        if t.ndim == 2:
            part = part.transpose(0, 2, 1, 3).reshape(n_dp * t.shape[0], n_mp * t.shape[1])
        else:
            part = part.transpose(2, 0, 3, 1, 4).reshape(t.shape[0], n_dp * t.shape[1], n_mp * t.shape[2])
        parts.append(part)

    layer_out, g_tokens, g_skip, big, little = item_compute(
        tokens_in, skip_tokens, cotangent, live, tuple(parts), small
    )

    big = (big[0], jnp.stack([b.astype(BF) for b in big[1]]), big[2], big[3], big[4])
    pieces = []
    for g, t in zip(big, tiles):
        g = g.astype(BF)
        if t.ndim == 2:
            g = g.reshape(n_dp, t.shape[0], n_mp, t.shape[1]).transpose(0, 2, 1, 3)
        else:
            g = g.reshape(t.shape[0], n_dp, t.shape[1], n_mp, t.shape[2]).transpose(1, 3, 0, 2, 4)
        pieces.append(g.reshape(n_dp * n_mp, -1, 384))
    sums = lax.psum_scatter(jnp.concatenate(pieces, axis=1), both, scatter_dimension=0, tiled=False)
    sums = sums.astype(F32)
    outs = []
    at = 0
    for t in tiles:
        count = t.size // 384
        outs.append(sums[at : at + count].reshape(t.shape))
        at += count

    little = jnp.concatenate(
        [jnp.stack(little[:9]).reshape(9, n_mp, cols).transpose(1, 0, 2), little[9].reshape(n_mp, 4, cols)], axis=1
    )
    little = lax.psum(little, both)
    little = lax.dynamic_slice_in_dim(little, column, 1, 0)[0]
    return (
        layer_out,
        g_tokens,
        g_skip,
        outs[0],
        little[0],
        little[1],
        little[2],
        outs[1].transpose(1, 0, 2),
        little[3:5],
        outs[2].T,
        little[5],
        little[6],
        little[7],
        outs[3],
        little[9:].reshape(-1),
        outs[4].T,
        little[8],
    )


def solution(mesh):
    in_specs = (
        P(("dp", "mp"), None),
        P(("dp", "mp"), None),
        P("dp"),
        P("dp", None),
        P("dp", "mp"),
        P("mp"),
        P("mp"),
        P("mp"),
        P("dp", None, "mp"),
        P(None, "mp"),
        P("mp", "dp"),
        P("mp"),
        P("mp"),
        P("mp"),
        P("dp", "mp"),
        P("mp"),
        P("mp", "dp"),
        P("mp"),
        P(("dp", "mp"), None),
    )
    out_specs = (
        P(("dp", "mp"), None),
        P(("dp", "mp"), None),
        P(("dp", "mp"), None),
        P("dp", "mp"),
        P("mp"),
        P("mp"),
        P("mp"),
        P("dp", None, "mp"),
        P(None, "mp"),
        P("mp", "dp"),
        P("mp"),
        P("mp"),
        P("mp"),
        P("dp", "mp"),
        P("mp"),
        P("mp", "dp"),
        P("mp"),
    )
    return jax.shard_map(local, mesh=mesh, in_specs=in_specs, out_specs=out_specs, check_vma=False)
```

time: 1030 us -> 640 us (0.62)
  waiting for transfers between devices: 663 us -> 229 us
  local copies, waits for them, and re-layouts: 44 us -> 243 us
  blocking collectives: 181 us -> 44.9 us
  other arithmetic: 24.6 us -> 13.4 us
  matrix products: 92.7 us -> 81.9 us
    reduce_scatter x9 -> x1, waiting for transfers between devices: 489 us -> 127 us  [local(): lax.psum_scatter(jnp.concatenate(pieces, axis=1), both, scatter_dimension...]
    reshape x1 -> x32, local copies, waits for them, and re-layouts: 2.36 us -> 119 us  [the longest x8 40.1 us: local(): g = g.reshape(n_dp, t.shape[0], n_mp, t.shape[1]).transpose(0, 2, 1, 3)]
    all_gather x3 -> x1, blocking collectives: 103 us -> 6.21 us  [local(): packed = lax.all_gather(packed, 'mp', axis=0)]
    all_gather x8 -> x1, waiting for transfers between devices: 145 us -> 102 us  [local(): gathered = lax.all_gather(flat, both, axis=0)]
    psum x5 -> x1, blocking collectives: 77.8 us -> 38.7 us  [local(): little = lax.psum(little, both)]
    slice x4 -> x23, local copies, waits for them, and re-layouts: 4.81 us -> 41.8 us  [the longest x4 18.2 us: local(): part = gathered[:, at:at + count].reshape((n_dp, n_mp) + t.shape)]
    unnamed x19 -> x2, waiting for transfers between devices: 28.6 us -> 0.03 us
    transpose x0 -> x6, local copies, waits for them, and re-layouts: none -> 20 us  [the longest x4 19.1 us: local(): part.transpose(0, 2, 1, 3).reshape(n_dp * t.shape[0], n_mp * t.shape[1])]
  transfers between devices with their start and end apart: 19 -> 2, of which waited for: 16 -> 2; matrix products, arithmetic and copies ran while one was open for 8% -> 5% of each run, Pallas kernels for 0% -> 0%
where the time goes in v1:
time: 640 us; the launch traced here: 628 us
  local copies, waits for them, and re-layouts  243 us (38%)
  waiting for transfers between devices  229 us (36%)
  matrix products  81.9 us (13%)
  blocking collectives  44.9 us (7%)
  between operations  15.2 us (2%)
  other arithmetic  13.4 us (2%)
    reduce_scatter x1, waiting for transfers between devices, local(): lax.psum_scatter(jnp.concatenate(pieces, axis=1), both, scatter_dimension...  127 us
    all_gather x1, waiting for transfers between devices, local(): gathered = lax.all_gather(flat, both, axis=0)  102 us
    reshape x8, local copies, waits for them, and re-layouts, local(): g = g.reshape(n_dp, t.shape[0], n_mp, t.shape[1]).transpose(0, 2, 1, 3)  40.1 us
    psum x1, blocking collectives, local(): little = lax.psum(little, both)  38.7 us
    reshape x5, local copies, waits for them, and re-layouts, local(): pieces.append(g.reshape(n_dp * n_mp, -1, 384))  30.8 us
    reshape x5, local copies, waits for them, and re-layouts, local(): part = gathered[:, at:at + count].reshape((n_dp, n_mp) + t.shape)  30.5 us
    unnamed x162, local copies, waits for them, and re-layouts  23.1 us
    dot_general x7, matrix products, rows_t(): lax.dot_general(a, b, (((0,), (0,)), ((), ())), preferred_element_type=F32)  20.9 us
  transfers between devices with their start and end apart: 2, of which 2 were waited for; matrix products, arithmetic and copies ran while one was open for 5% of the time, Pallas kernels for 0%

profile of v1, /device:TPU:0, one launch (start us, length us, event | category | flops | bytes accessed | tf_op | source)
XLA Modules:
  0.0 627.7 jit_solution(17813266530321201058)
XLA Ops:
  13.7 6.2 all-gather.2
  27.8 101.8 %all-gather.5.cloned.1.call-done = bf16[21504,384]{1,0:T(8,128)(2,1)} async-done(((bf16[672,384]{1,0:T(8,128)(2,1)}), bf16[21504,384]{1,0:T(8,128)(2,1)}) %all-gather.5.cloned.1.call-update) | async-done | bytes 16515088 | tf_op jit(solution)/shard_map/all_gather | solution.py:177
  139.5 8.4 %fusion.43 = (bf16[32,192,384]{2,1,0:T(8,128)(2,1)}, bf16[32,192,384]{2,1,0:T(8,128)(2,1)}) fusion(bf16[32,672,384]{2,1,0:T(8,128)(2,1)} %bitcast.178), kind=kLoop, calls=%fused_computation.136 | loop fusion | bytes 18874368 | tf_op jit(solution)/shard_map/slice | solution.py:182
  147.9 4.6 reshape.386
  156.8 6.0 reshape.387
  162.8 7.7 %reshape.388 = bf16[8,4,3,96,192]{4,3,2,1,0:T(8,128)(2,1)} reshape(bf16[32,144,384]{2,1,0:T(8,128)(2,1)} %slice.220) | data formatting | bytes 7077888 | tf_op jit(solution)/shard_map/reshape | solution.py:182
  170.5 4.6 fusion.44
  212.5 8.4 %reshape.395 = bf16[8,4,96,768]{3,2,1,0:T(8,128)(2,1)} reshape(bf16[32,192,384]{2,1,0:T(8,128)(2,1)} %get-tuple-element.96) | data formatting | bytes 9437184 | tf_op jit(solution)/shard_map/reshape | solution.py:182
  221.0 6.0 copy.102
  230.2 8.0 %reshape.397 = bf16[8,4,96,768]{3,2,1,0:T(8,128)(2,1)} reshape(bf16[32,192,384]{2,1,0:T(8,128)(2,1)} %get-tuple-element.95) | data formatting | bytes 9437184 | tf_op jit(solution)/shard_map/reshape | solution.py:182
  238.2 6.0 copy.103
  247.4 7.4 %fusion.48 = (f32[12,384]{1,0:T(8,128)}, f32[12,384,384]{1,2,0:T(8,128)}) fusion(pred[384]{0:T(512)(128)(4,1)S(1)} %copy-done.61, bf16[384,12,64]{0,2,1:T(8,128)(2,1)S(1)} %bitcast.194, bf16[384,12,64]{0,2,1:T(8,128)(2,1)} %bitcast.196), kind=kOutput, calls=%fused_computation.141 | convolution fusion | flops 233570688 | bytes 8276352 | tf_op jit(solution)/shard_map/sub | solution.py:68
  263.6 6.2 convert_reduce_fusion
  277.4 7.1 %multiply_reduce_fusion = (f32[12,384]{1,0:T(8,128)S(1)}, f32[12,384,384]{1,2,0:T(8,128)}) fusion(f32[12,384,384]{1,2,0:T(8,128)} %get-tuple-element.122, f32[12,384]{1,0:T(8,128)} %get-tuple-element.121, bf16[384,12,64]{0,2,1:T(8,128)(2,1)S(1)} %bitcast.202, bf16[384,12,64]{0,2,1:T(8,128)(2,1)} %bitcast.201), kind=kOutput, calls=%fused_computation.2 | convolution fusion | flops 231796224 | bytes 15372288 | tf_op jit(solution)/shard_map/isha,itha->ihst/dot_general | solution.py:97
  284.5 6.3 multiply_convert_fusion
  293.3 4.6 convert_reduce_fusion.3
  302.6 4.9 convolution_convert_fusion.1
  318.5 6.1 reshape.403
  326.7 4.6 reshape.404
  336.8 4.4 stack.76
  342.9 4.8 stack.75
  352.1 7.9 %reshape.405 = bf16[32,144,384]{2,1,0:T(8,128)(2,1)} reshape(bf16[8,4,3,96,192]{4,3,2,1,0:T(8,128)(2,1)} %maximum_bitcast_fusion) | data formatting | bytes 7077888 | tf_op jit(solution)/shard_map/reshape | solution.py:202
  363.5 9.7 %reshape.408 = bf16[8,96,4,768]{3,2,1,0:T(4,128)(2,1)} reshape(bf16[768,3072]{1,0:T(8,128)(2,1)} %convolution_convert_fusion.1) | data formatting | bytes 9437184 | tf_op jit(solution)/shard_map/reshape | solution.py:199
  373.3 5.4 copy.129
  378.6 8.2 %reshape.409 = bf16[32,192,384]{2,1,0:T(8,128)(2,1)} reshape(bf16[8,4,96,768]{3,2,1,0:T(8,128)(2,1)} %bitcast.172) | data formatting | bytes 9437184 | tf_op jit(solution)/shard_map/reshape | solution.py:202
  386.9 4.5 convolution_convert_fusion
  391.4 9.7 %reshape.410 = bf16[8,96,4,768]{3,2,1,0:T(4,128)(2,1)} reshape(bf16[768,3072]{1,0:T(8,128)(2,1)} %convolution_convert_fusion) | data formatting | bytes 9437184 | tf_op jit(solution)/shard_map/reshape | solution.py:199
  401.1 5.4 copy.128
  406.4 8.2 %reshape.411 = bf16[32,192,384]{2,1,0:T(8,128)(2,1)} reshape(bf16[8,4,96,768]{3,2,1,0:T(8,128)(2,1)} %bitcast.173) | data formatting | bytes 9437184 | tf_op jit(solution)/shard_map/reshape | solution.py:202
  436.7 38.7 %psum.7 = f32[4,13,192]{2,1,0:T(8,128)S(1)} all-reduce(f32[4,13,192]{2,1,0:T(8,128)S(1)} %pad_maximum_fusion), channel_id=1, replica_groups=mesh['dp'=8,'mp'=4] {'dp','mp'}, use_global_device_ids=true, to_apply=%region_22.23 | all-reduce | flops 9984 | bytes 79872 | tf_op jit(solution)/shard_map/psum | solution.py:215
  482.1 5.2 fusion.18
  487.2 127.5 %reduce-scatter.2.cloned.1.call-done = bf16[1,672,384]{2,1,0:T(8,128)(2,1)} async-done(((bf16[32,672,384]{2,1,0:T(8,128)(2,1)}), bf16[1,672,384]{2,1,0:T(8,128)(2,1)}) %reduce-scatter.2.cloned.1.call-update) | async-done | bytes 516112 | tf_op jit(solution)/shard_map/reduce_scatter | solution.py:203
  (288 shorter events, 158.1 us)
Async XLA Ops:
  7.2 6.3 copy-start.44
  7.2 6.3 %copy-start.54 = (f32[192]{0:T(256)S(1)}, f32[192]{0:T(256)}, u32[]{:S(2)}) copy-start(f32[192]{0:T(256)} %param.24) | copy-start | bytes 2308
  7.2 6.3 %copy-start.55 = (f32[192]{0:T(256)S(1)}, f32[192]{0:T(256)}, u32[]{:S(2)}) copy-start(f32[192]{0:T(256)} %param.25) | copy-start | bytes 2308
  7.2 6.3 %copy-start.56 = (f32[192]{0:T(256)S(1)}, f32[192]{0:T(256)}, u32[]{:S(2)}) copy-start(f32[192]{0:T(256)} %param.26) | copy-start | bytes 2308
  7.2 6.3 %copy-start.53 = (f32[2,192]{1,0:T(2,128)S(1)}, f32[2,192]{1,0:T(2,128)}, u32[]{:S(2)}) copy-start(f32[2,192]{1,0:T(2,128)} %param.28) | copy-start | bytes 4612
  7.2 6.3 %copy-start.57 = (f32[192]{0:T(256)S(1)}, f32[192]{0:T(256)}, u32[]{:S(2)}) copy-start(f32[192]{0:T(256)} %param.30) | copy-start | bytes 2308
  7.3 6.3 %copy-start.58 = (f32[192]{0:T(256)S(1)}, f32[192]{0:T(256)}, u32[]{:S(2)}) copy-start(f32[192]{0:T(256)} %param.31) | copy-start | bytes 2308
  7.3 6.3 %copy-start.59 = (f32[192]{0:T(256)S(1)}, f32[192]{0:T(256)}, u32[]{:S(2)}) copy-start(f32[192]{0:T(256)} %param.32) | copy-start | bytes 2308
  7.3 6.3 %copy-start.60 = (f32[192]{0:T(256)S(1)}, f32[192]{0:T(256)}, u32[]{:S(2)}) copy-start(f32[192]{0:T(256)} %param.36) | copy-start | bytes 2308
  7.3 122.4 %all-gather.5.cloned.1.call-start = ((), (), s32[]{:S(2)}) async-start(), calls=%async_computation.2 | async-start | bytes 17031168 | tf_op jit(solution)/shard_map/all_gather | solution.py:177
  8.4 15.3 %copy-start.62 = (s32[4]{0:T(128)S(1)}, s32[4]{0:T(128)}, u32[]{:S(2)}) copy-start(s32[4]{0:T(128)} %param.21) | copy-start | bytes 52
  8.4 15.9 %copy-start.52 = (s32[4,77]{1,0:T(4,128)S(1)}, s32[4,77]{1,0:T(4,128)}, u32[]{:S(2)}) copy-start(s32[4,77]{1,0:T(4,128)} %param.22) | copy-start | bytes 3700
  8.4 17.8 %copy-start.26 = (bf16[384,768]{1,0:T(8,128)(2,1)S(1)}, bf16[384,768]{1,0:T(8,128)(2,1)}, u32[]{:S(2)}) copy-start(bf16[384,768]{1,0:T(8,128)(2,1)} %param.19) | copy-start | bytes 1769476
  12.5 14.5 %copy-start.27 = (bf16[384,768]{1,0:T(8,128)(2,1)S(1)}, bf16[384,768]{1,0:T(8,128)(2,1)}, u32[]{:S(2)}) copy-start(bf16[384,768]{1,0:T(8,128)(2,1)} %param.20) | copy-start | bytes 1769476
  13.4 601.3 %reduce-scatter.2.cloned.1.call-start = ((), (), s32[]{:S(2)}) async-start(), calls=%async_computation.1 | async-start | bytes 17031168 | tf_op jit(solution)/shard_map/reduce_scatter | solution.py:203
  23.7 246.1 %copy-start.33 = (f32[768]{0:T(1024)}, f32[768]{0:T(1024)S(1)}, u32[]{:S(2)}) copy-start(f32[768]{0:T(1024)S(1)} %mul.210) | copy-start | bytes 9220
  25.0 107.9 %copy-start.42 = (f32[384]{0:T(512)}, f32[384]{0:T(512)S(1)}, u32[]{:S(2)}) copy-start(f32[384]{0:T(512)S(1)} %get-tuple-element.93) | copy-start | bytes 4612
  182.8 17.2 %copy-start.2 = (bf16[384,768]{1,0:T(8,128)(2,1)}, bf16[384,768]{1,0:T(8,128)(2,1)S(1)}, u32[]{:S(2)}) copy-start(bf16[384,768]{1,0:T(8,128)(2,1)S(1)} %add_convert_fusion.2) | copy-start | bytes 1769476
  193.1 54.2 %copy-start.17 = (bf16[384,768]{0,1:T(8,128)(2,1)}, bf16[384,768]{0,1:T(8,128)(2,1)S(1)}, u32[]{:S(2)}) copy-start(bf16[384,768]{0,1:T(8,128)(2,1)S(1)} %copy.97) | copy-start | bytes 1769476
  247.4 12.3 %slice-start.6 = ((s8[4718592]{0:T(1024)(128)(4,1)}), s8[524288]{0:T(1024)(128)(4,1)S(1)}, s32[]{:S(2)}) async-start(s8[4718592]{0:T(1024)(128)(4,1)} %bitcast.190), calls=%async_computation.9 | async-start | bytes 1048576
  259.6 13.0 %copy-start.9 = (f32[384,768]{1,0:T(8,128)}, f32[384,768]{1,0:T(8,128)S(1)}, u32[]{:S(2)}) copy-start(f32[384,768]{1,0:T(8,128)S(1)} %get-tuple-element.123) | copy-start | bytes 3538948
  259.6 13.0 %copy-start.38 = (f32[384]{0:T(512)}, f32[384]{0:T(512)S(1)}, u32[]{:S(2)}) copy-start(f32[384]{0:T(512)S(1)} %get-tuple-element.116) | copy-start | bytes 4612
  259.6 13.0 %copy-start.40 = (f32[384]{0:T(512)}, f32[384]{0:T(512)S(1)}, u32[]{:S(2)}) copy-start(f32[384]{0:T(512)S(1)} %get-tuple-element.117) | copy-start | bytes 4612
  277.3 7.2 %copy-start.30 = (f32[12,384]{1,0:T(8,128)S(1)}, f32[12,384]{1,0:T(8,128)}, u32[]{:S(2)}) copy-start(f32[12,384]{1,0:T(8,128)} %get-tuple-element.121) | copy-start | bytes 55300
  284.5 6.3 %copy-start.19 = (bf16[384,768]{0,1:T(8,128)(2,1)S(1)}, bf16[384,768]{0,1:T(8,128)(2,1)}, u32[]{:S(2)}) copy-start(bf16[384,768]{0,1:T(8,128)(2,1)} %copy.99) | copy-start | bytes 1769476
  352.1 7.9 %copy-start.16 = (bf16[768,768]{1,0:T(8,128)(2,1)S(1)}, bf16[768,768]{1,0:T(8,128)(2,1)}, u32[]{:S(2)}) copy-start(bf16[768,768]{1,0:T(8,128)(2,1)} %convolution_convert_fusion.3) | copy-start | bytes 3538948
  378.6 8.2 %copy-start.29 = (bf16[384,768]{1,0:T(8,128)(2,1)S(1)}, bf16[384,768]{1,0:T(8,128)(2,1)}, u32[]{:S(2)}) copy-start(bf16[384,768]{1,0:T(8,128)(2,1)} %param.37) | copy-start | bytes 1769476
  378.6 8.2 %copy-start.51 = (bf16[384]{0:T(512)(128)(2,1)S(1)}, bf16[384]{0:T(512)(128)(2,1)}, u32[]{:S(2)}) copy-start(bf16[384]{0:T(512)(128)(2,1)} %convert_element_type.157) | copy-start | bytes 2308
  378.6 8.2 %copy-start.63 = (bf16[384,3072]{1,0:T(8,128)(2,1)S(1)}, bf16[384,3072]{1,0:T(8,128)(2,1)}, u32[]{:S(2)}) copy-start(bf16[384,3072]{1,0:T(8,128)(2,1)} %get-tuple-element.124) | copy-start | bytes 7077892
  406.4 13.7 %slice-start = ((s8[4718592]{0:T(1024)(128)(4,1)}), s8[524288]{0:T(1024)(128)(4,1)S(1)}, s32[]{:S(2)}) async-start(s8[4718592]{0:T(1024)(128)(4,1)} %bitcast.164), calls=%async_computation.3 | async-start | bytes 1048576
  433.5 43.8 %copy-start.6 = (bf16[384,768]{1,0:T(8,128)(2,1)S(1)}, bf16[384,768]{1,0:T(8,128)(2,1)}, u32[]{:S(2)}) copy-start(bf16[384,768]{1,0:T(8,128)(2,1)} %copy-done.5) | copy-start | bytes 1769476
  436.7 43.7 %copy-start.15 = (bf16[768,768]{1,0:T(8,128)(2,1)S(1)}, bf16[768,768]{1,0:T(8,128)(2,1)}, u32[]{:S(2)}) copy-start(bf16[768,768]{1,0:T(8,128)(2,1)} %slice.199) | copy-start | bytes 3538948
  (45 other events, 127.4 us)
Sparse Core Ops, SparseCore 0:
  13.5 116.0 all-gather.4
  425.6 189.0 reduce-scatter.1

commit v2 on v1

--- a/solution.py
+++ b/solution.py
@@ -1,8 +1,11 @@
+import functools
 import math
 
 import jax
 import jax.numpy as jnp
 from jax import lax
+from jax.experimental import pallas as pl
+from jax.experimental.pallas import tpu as pltpu
 from jax.sharding import PartitionSpec as P
 
 HEAD = 64
@@ -134,6 +137,230 @@
     return jnp.where(positions[None, :] < LAT, 1, caption_flag[:, None] * padded)
 
 
+MESH = pl.DeviceIdType.MESH
+LANES = 384
+PIECES = 5
+
+
+def piece_view(flavour, piece, arrays, dp, y, core):
+    w_skip, w_qkv, w_out_t, w_up, w_down_t = arrays
+    cols = pl.ds(pl.multiple_of(y * LANES, 128), LANES)
+    if piece == 0:
+        rows = w_skip.shape[0] // 8
+        start = dp * rows + core * (rows // 2) + flavour * (rows // 4)
+        return w_skip.at[pl.ds(pl.multiple_of(start, 16), rows // 4), cols]
+    if piece in (1, 2):
+        rows = w_out_t.shape[0] // 8
+        span = pl.ds(pl.multiple_of(dp * rows + core * (rows // 2), 16), rows // 2)
+        if flavour == 1 and piece == 2:
+            return w_out_t.at[span, cols]
+        return w_qkv.at[2 if flavour == 1 else piece - 1, span, cols]
+    array = w_up if piece == 3 else w_down_t
+    rows = array.shape[0] // 8
+    start = y * (4 * LANES) + core * (2 * LANES) + flavour * LANES
+    return array.at[pl.ds(pl.multiple_of(dp * rows, 16), rows), pl.ds(pl.multiple_of(start, 128), LANES)]
+
+
+def own_view(flavour, piece, merged, up, down):
+    half = merged.shape[0] // 6
+    if piece == 0:
+        return merged.at[pl.ds(flavour * half, half)]
+    if piece in (1, 2):
+        order = ((2, 3), (4, 5))[flavour]
+        return merged.at[pl.ds(order[piece - 1] * half, half)]
+    return (up if piece == 3 else down).at[:, pl.ds(flavour * LANES, LANES)]
+
+
+def gather_kernel(
+    narrow, up, down, little,
+    w_skip, w_qkv, w_out_t, w_up, w_down_t, little_all,
+    merged, other, own_sem, pair_sem, little_sem, z_sem, a_sem, b_sem, c_sem,
+):
+    dp, mp = lax.axis_index("dp"), lax.axis_index("mp")
+    z, x, y, core = dp // 2, dp % 2, mp // 2, mp % 2
+    arrays = (w_skip, w_qkv, w_out_t, w_up, w_down_t)
+
+    def device(zz, xx, yy, cc):
+        return (zz * 2 + xx, yy * 2 + cc)
+
+    z_others = [(z + d) % 4 for d in (1, 2, 3)]
+    partner = device(z, x, y, 1 - core)
+    across = [device(z, x, 1 - y, core), device(z, x, 1 - y, 1 - core)]
+    beside = device(z, 1 - x, y, core)
+    barrier = pltpu.get_barrier_semaphore()
+    friends = [device(zz, x, y, core) for zz in z_others] + [partner, beside] + across
+    for friend in friends:
+        pl.semaphore_signal(barrier, inc=1, device_id=friend, device_id_type=MESH)
+    pl.semaphore_wait(barrier, len(friends))
+
+    def remote(source, target, sems, index, to):
+        return pltpu.make_async_remote_copy(
+            src_ref=source,
+            dst_ref=target,
+            send_sem=sems.at[(0,) + index],
+            recv_sem=sems.at[(1,) + index],
+            device_id=to,
+            device_id_type=MESH,
+        )
+
+    swap = remote(narrow.at[1 - core], other, pair_sem, (), partner)
+    swap.start()
+    pltpu.make_async_copy(little, little_all.at[mp], own_sem.at[2 * PIECES]).start()
+    for i, to in enumerate([partner] + across):
+        remote(little, little_all.at[mp], little_sem, (i,), to).start()
+
+    def forward(flavour, piece, source, zz, xx, yy, stage):
+        view = piece_view(flavour, piece, arrays, zz * 2 + xx, yy, core)
+        source = view if source is None else source
+        side = xx if flavour == 0 else yy
+        if stage == 1:
+            remote(source, view, a_sem, (flavour, piece, zz), (beside, across[0])[flavour]).start()
+        if stage <= 2:
+            remote(source, view, b_sem, (flavour, piece, side * 4 + zz), (across[0], beside)[flavour]).start()
+        remote(source, view, c_sem, (flavour, piece, (xx * 2 + yy) * 4 + zz), partner).start()
+
+    def start_own(flavour, piece):
+        source = own_view(flavour, piece, merged, up, down)
+        view = piece_view(flavour, piece, arrays, dp, y, core)
+        pltpu.make_async_copy(source, view, own_sem.at[flavour * PIECES + piece]).start()
+        for i, zz in enumerate(z_others):
+            pltpu.make_async_remote_copy(
+                src_ref=source, dst_ref=view,
+                send_sem=z_sem.at[0, flavour, piece, i],
+                recv_sem=z_sem.at[1, flavour, piece, z],
+                device_id=device(zz, x, y, core), device_id_type=MESH,
+            ).start()
+        forward(flavour, piece, source, z, x, y, 1)
+
+    def arrived(flavour, piece, zz, xx, yy, sems, index):
+        view = piece_view(flavour, piece, arrays, zz * 2 + xx, yy, core)
+        remote(view, view, sems, index, partner).wait_recv()
+
+    remote(narrow.at[0], other, pair_sem, (), partner).wait_recv()
+    mine, theirs = narrow[core], other[...]
+    lead = jnp.where(core == 0, mine, theirs)
+    tail = jnp.where(core == 0, theirs, mine)
+    merged[...] = jnp.concatenate([lead, tail], axis=1)
+    for piece in range(PIECES):
+        for flavour in (0, 1):
+            start_own(flavour, piece)
+
+    def stage_z(piece):
+        for flavour in (0, 1):
+            for zz in z_others:
+                arrived(flavour, piece, zz, x, y, z_sem, (flavour, piece, zz))
+                forward(flavour, piece, None, zz, x, y, 1)
+
+    def stage_a(piece):
+        for zz in [z] + z_others:
+            for flavour in (0, 1):
+                xx, yy = ((1 - x, y), (x, 1 - y))[flavour]
+                arrived(flavour, piece, zz, xx, yy, a_sem, (flavour, piece, zz))
+                forward(flavour, piece, None, zz, xx, yy, 2)
+
+    def stage_b(piece):
+        for near in (0, 1):
+            for zz in [z] + z_others:
+                for flavour in (0, 1):
+                    if flavour == 0:
+                        xx, yy = (x if near == 0 else 1 - x), 1 - y
+                        side = xx
+                    else:
+                        xx, yy = 1 - x, (y if near == 0 else 1 - y)
+                        side = yy
+                    arrived(flavour, piece, zz, xx, yy, b_sem, (flavour, piece, side * 4 + zz))
+                    forward(flavour, piece, None, zz, xx, yy, 3)
+
+    for step in range(PIECES + 2):
+        if step < PIECES:
+            stage_z(step)
+        if 1 <= step <= PIECES:
+            stage_a(step - 1)
+        if step >= 2:
+            stage_b(step - 2)
+
+    swap.wait_send()
+    pltpu.make_async_copy(little, little_all.at[mp], own_sem.at[2 * PIECES]).wait()
+    for i, to in enumerate([partner] + across):
+        copy = remote(little, little_all.at[0], little_sem, (i,), to)
+        copy.wait_send()
+        copy.wait_recv()
+    for flavour in (0, 1):
+        for piece in range(PIECES):
+            view = piece_view(flavour, piece, arrays, dp, y, core)
+            pltpu.make_async_copy(
+                own_view(flavour, piece, merged, up, down), view, own_sem.at[flavour * PIECES + piece]
+            ).wait()
+            for i in range(3):
+                remote(view, view, z_sem, (flavour, piece, i), partner).wait_send()
+            for i in range(4):
+                remote(view, view, a_sem, (flavour, piece, i), partner).wait_send()
+            for i in range(8):
+                remote(view, view, b_sem, (flavour, piece, i), partner).wait_send()
+            for i in range(16):
+                copy = remote(view, view, c_sem, (flavour, piece, i), partner)
+                copy.wait_send()
+                copy.wait_recv()
+
+
+def gather_weights(w_skip, w_qkv, w_out, w_up, w_down, little):
+    def halves(tile):
+        return tile.reshape(2, tile.shape[0] // 2, tile.shape[1])
+
+    width = w_qkv.shape[0] * 8
+    narrow = jnp.concatenate(
+        [halves(w_skip)] + [halves(w_qkv[:, t]) for t in range(3)] + [halves(w_out.T)], axis=1
+    )
+    hidden = w_up.shape[1] * 4
+    dma = pltpu.SemaphoreType.DMA
+    any_space = pl.BlockSpec(memory_space=pl.ANY)
+    vmem = pl.BlockSpec(memory_space=pltpu.VMEM)
+    shape = jax.ShapeDtypeStruct
+    return pl.pallas_call(
+        gather_kernel,
+        out_shape=(
+            shape((2 * width, width), BF),
+            shape((3, width, width), BF),
+            shape((width, width), BF),
+            shape((width, hidden), BF),
+            shape((width, hidden), BF),
+            shape((4,) + little.shape, F32),
+        ),
+        in_specs=[vmem] * 4,
+        out_specs=(any_space,) * 6,
+        scratch_shapes=[
+            pltpu.VMEM((narrow.shape[1], LANES), BF),
+            pltpu.VMEM(narrow.shape[1:], BF),
+            dma((2 * PIECES + 1,)),
+            dma((2,)),
+            dma((2, 3)),
+            dma((2, 2, PIECES, 4)),
+            dma((2, 2, PIECES, 4)),
+            dma((2, 2, PIECES, 8)),
+            dma((2, 2, PIECES, 16)),
+        ],
+        compiler_params=pltpu.CompilerParams(collective_id=0, has_side_effects=True),
+        name="gather_weights",
+    )(narrow, w_up, w_down.T, little)
+
+
+def whole_tiles(tiles, n_dp, n_mp):
+    flat = jnp.concatenate([t.reshape(-1, 384) for t in tiles], axis=0)
+    gathered = lax.all_gather(flat, ("dp", "mp"), axis=0)
+    parts = []
+    at = 0
+    for t in tiles:
+        count = t.size // 384
+        part = gathered[:, at : at + count].reshape((n_dp, n_mp) + t.shape)
+        at += count
+        if t.ndim == 2:
+            part = part.transpose(0, 2, 1, 3).reshape(n_dp * t.shape[0], n_mp * t.shape[1])
+        else:
+            part = part.transpose(2, 0, 3, 1, 4).reshape(t.shape[0], n_dp * t.shape[1], n_mp * t.shape[2])
+        parts.append(part)
+    return parts
+
+
 def local(
     tokens_in,
     skip_tokens,
@@ -168,24 +395,17 @@
         [b_skip, gain_attn, shift_attn, b_qv[0], b_qv[1], b_out, gain_mlp, shift_mlp, b_down]
         + [b_up.reshape(4, -1)[i] for i in range(4)]
     )
-    packed = lax.all_gather(packed, "mp", axis=0)
+    tiles = (w_skip, w_qkv.transpose(1, 0, 2), w_out.T, w_up, w_down.T)
+    fast = (n_dp, n_mp, cols) == (8, 4, 192) and w_up.shape == (96, 768)
+    if fast:
+        padded = jnp.pad(packed, ((0, 3), (0, 64)))
+        *parts, packed = gather_weights(w_skip, w_qkv, w_out, w_up, w_down, padded)
+        packed = packed[:, :13, :cols]
+    else:
+        packed = lax.all_gather(packed, "mp", axis=0)
+        parts = whole_tiles(tiles, n_dp, n_mp)
     whole = packed[:, :9].transpose(1, 0, 2).reshape(9, -1)
     small = tuple(whole[i] for i in range(9)) + (packed[:, 9:].reshape(-1),)
-
-    tiles = (w_skip, w_qkv.transpose(1, 0, 2), w_out.T, w_up, w_down.T)
-    flat = jnp.concatenate([t.reshape(-1, 384) for t in tiles], axis=0)
-    gathered = lax.all_gather(flat, both, axis=0)
-    parts = []
-    at = 0
-    for t in tiles:
-        count = t.size // 384
-        part = gathered[:, at : at + count].reshape((n_dp, n_mp) + t.shape)
-        at += count
-        if t.ndim == 2:
-            part = part.transpose(0, 2, 1, 3).reshape(n_dp * t.shape[0], n_mp * t.shape[1])
-        else:
-            part = part.transpose(2, 0, 3, 1, 4).reshape(t.shape[0], n_dp * t.shape[1], n_mp * t.shape[2])
-        parts.append(part)
 
     layer_out, g_tokens, g_skip, big, little = item_compute(
         tokens_in, skip_tokens, cotangent, live, tuple(parts), small

time: 640 us -> 528 us (0.82)
  local copies, waits for them, and re-layouts: 243 us -> 134 us
  waiting for transfers between devices: 229 us -> 138 us
  Pallas kernels: 0 us -> 85.6 us
  matrix products: 81.9 us -> 90.8 us
    all_gather x1 -> x0, waiting for transfers between devices: 102 us -> none  [local(): gathered = lax.all_gather(flat, both, axis=0)]
    pallas_call x0 -> x1, Pallas kernels: none -> 85.6 us  [gather_weights(): pl.pallas_call(gather_kernel, out_shape=(shape((2 * width, width), BF), s...]
    reshape x12 -> x0, local copies, waits for them, and re-layouts: 43.7 us -> none  [the longest x5 30.5 us: local(): part = gathered[:, at:at + count].reshape((n_dp, n_mp) + t.shape)]
    slice x13 -> x1, local copies, waits for them, and re-layouts: 38 us -> 0.86 us  [gather_weights(): w_qkv[:, t]]
    transpose x5 -> x1, local copies, waits for them, and re-layouts: 20 us -> 0.89 us  [gather_weights(): narrow = jnp.concatenate([halves(w_skip)] + [halves(w_qkv[:, t]) for t in...]
    reduce_scatter x1, waiting for transfers between devices: 127 us -> 138 us  [local(): lax.psum_scatter(jnp.concatenate(pieces, axis=1), both, scatter_dimension...]
    unnamed x162 -> x140, local copies, waits for them, and re-layouts: 23.1 us -> 13.9 us
    squeeze x3 -> x0, local copies, waits for them, and re-layouts: 8.89 us -> none  [the longest x1 3.8 us: item_compute(): k = split(mm(n1, w_qkv[1]).astype(BF))]
  transfers between devices with their start and end apart: 2 -> 1, of which waited for: 2 -> 1; matrix products, arithmetic and copies ran while one was open for 5% -> 2% of each run, Pallas kernels for 0% -> 0%
where the time goes in v2:
time: 528 us; the launch traced here: 519 us
  waiting for transfers between devices  138 us (26%)
  local copies, waits for them, and re-layouts  134 us (25%)
  matrix products  90.8 us (17%)
  Pallas kernels  85.6 us (16%)
  blocking collectives  42 us (8%)
  between operations  15.3 us (3%)
  other arithmetic  14 us (3%)
    reduce_scatter x1, waiting for transfers between devices, local(): lax.psum_scatter(jnp.concatenate(pieces, axis=1), both, scatter_dimension...  138 us
    pallas_call x1, Pallas kernels, gather_weights(): pl.pallas_call(gather_kernel, out_shape=(shape((2 * width, width), BF), s...  85.6 us
    reshape x8, local copies, waits for them, and re-layouts, local(): g = g.reshape(n_dp, t.shape[0], n_mp, t.shape[1]).transpose(0, 2, 1, 3)  45.7 us
    psum x1, blocking collectives, local(): little = lax.psum(little, both)  42 us
    reshape x5, local copies, waits for them, and re-layouts, local(): pieces.append(g.reshape(n_dp * n_mp, -1, 384))  30.9 us
    dot_general x7, matrix products, rows_t(): lax.dot_general(a, b, (((0,), (0,)), ((), ())), preferred_element_type=F32)  29.5 us
    dot_general x7, matrix products, mm(): return jnp.dot(a, b, preferred_element_type=F32)  21.3 us
    another operation x6, local copies, waits for them, and re-layouts, local(): jnp.stack([b.astype(BF) for b in big[1]])  16.2 us
  transfers between devices with their start and end apart: 1, of which 1 were waited for; matrix products, arithmetic and copies ran while one was open for 2% of the time, Pallas kernels for 0%

profile of v2, /device:TPU:0, one launch (start us, length us, event | category | flops | bytes accessed | tf_op | source)
XLA Modules:
  0.0 519.3 jit_solution(8690066006963494848)
XLA Ops:
  13.7 85.6 %gather_weights.1 = (bf16[1536,768]{1,0:T(8,128)(2,1)}, bf16[3,768,768]{2,1,0:T(8,128)(2,1)}, bf16[768,768]{1,0:T(8,128)(2,1)}, bf16[768,3072]{1,0:T(8,128)(2,1)...) custom-call(bf16[2,288,192]{2,1,0:T(8,128)(2,1)} %copy-done.20, bf16[96,768]{1,0:T(8,128)(2,1)} %up.1, ...), custom_call_target="tpu_custom_call" | custom-call | tf_op jit(solution)/shard_map/gather_weights/pallas_call | solution.py:319
  103.8 3.3 fusion.59
  119.2 6.1 %fusion.63 = (f32[12,384]{1,0:T(8,128)}, f32[12,384,384]{1,2,0:T(8,128)}) fusion(pred[384]{0:T(512)(128)(4,1)} %compare_reduce_fusion, bf16[384,12,64]{0,2,1:T(8,128)(2,1)S(1)} %bitcast.152, bf16[384,12,64]{0,2,1:T(8,128)(2,1)S(1)} %bitcast.154), kind=kOutput, calls=%fused_computation.156 | convolution fusion | flops 233570688 | bytes 8276352 | tf_op jit(solution)/shard_map/sub | solution.py:71
  125.3 3.8 fusion.23
  130.1 6.4 %multiply_convert_fusion.1 = (bf16[384,3072]{1,0:T(8,128)(2,1)}, f32[384,3072]{1,0:T(8,128)S(1)}) fusion(f32[3072]{0:T(1024)S(1)} %copy-done.37, bf16[768,3072]{1,0:T(8,128)(2,1)} %get-tuple-element.27, f32[384,768]{1,0:T(8,128)S(1)} %get-tuple-element.97, f32[768]{0:T(1024)S(1)} %add.152, f32[768]{0:T(1024)S(1)} %mul.210, f32[384]{0:T(512)S(1)} %get-tuple-element.91, ...), kind=kOutput, calls=%fused_computation.19 | convolution fusion | flops 1820491776 | bytes 12997632 | tf_op jit(solution)/shard_map/dot_general | solution.py:30
  136.6 6.0 %convert_reduce_fusion = (f32[3072]{0:T(1024)}, bf16[384,3072]{1,0:T(8,128)(2,1)S(1)}) fusion(f32[384,3072]{1,0:T(8,128)S(1)} %get-tuple-element.99, bf16[768,3072]{1,0:T(8,128)(2,1)S(1)} %bitcast.194, bf16[384,768]{1,0:T(8,128)(2,1)S(1)} %copy-done.19, bf16[384]{0:T(512)(128)(2,1)S(1)} %convert_element_type.159), kind=kOutput, calls=%fused_computation.18 | convolution fusion | flops 1826386944 | bytes 12399360 | tf_op jit(solution)/shard_map/dot_general | solution.py:30
  142.6 2.8 multiply_reduce_fusion.1
  149.7 7.5 %multiply_reduce_fusion = (f32[12,384]{1,0:T(8,128)S(1)}, f32[12,384,384]{1,2,0:T(8,128)}) fusion(f32[12,384,384]{1,2,0:T(8,128)} %get-tuple-element.96, f32[12,384]{1,0:T(8,128)} %get-tuple-element.95, bf16[384,12,64]{0,2,1:T(8,128)(2,1)} %bitcast.160, bf16[384,12,64]{0,2,1:T(8,128)(2,1)} %bitcast.159), kind=kOutput, calls=%fused_computation.2 | convolution fusion | flops 231796224 | bytes 15372288 | tf_op jit(solution)/shard_map/isha,itha->ihst/dot_general | solution.py:100
  157.2 6.3 %multiply_convert_fusion = bf16[12,384,384]{1,2,0:T(8,128)(2,1)S(1)} fusion(f32[12,384,384]{1,2,0:T(8,128)} %get-tuple-element.102, f32[12,384]{1,0:T(8,128)S(1)} %get-tuple-element.101, f32[12,384,384]{1,2,0:T(8,128)} %get-tuple-element.96, f32[12,384]{1,0:T(8,128)S(1)} %copy-done.25), kind=kLoop, calls=%fused_computation.1 | loop fusion | flops 7077888 | bytes 17731584 | tf_op jit(solution)/shard_map/convert_element_type | solution.py:102
  165.7 5.2 %convert_reduce_fusion.3 = (f32[12,64]{1,0:T(8,128)}, bf16[12,64,384]{2,1,0:T(8,128)(2,1)S(1)}) fusion(bf16[384,12,64]{0,2,1:T(8,128)(2,1)S(1)} %bitcast.161, f32[12,384,384]{1,2,0:T(8,128)} %get-tuple-element.96, f32[12,384]{1,0:T(8,128)S(1)} %copy-done.25), kind=kOutput, calls=%fused_computation.69 | convolution fusion | flops 230915328 | bytes 8279040 | tf_op jit(solution)/shard_map/ihst,isha->itha/dot_general | solution.py:105
  175.4 12.5 %convolution_convert_fusion.1 = bf16[768,3072]{1,0:T(8,128)(2,1)} fusion(bf16[384,3072]{1,0:T(8,128)(2,1)S(1)} %copy-done.58, f32[384,768]{1,0:T(8,128)S(1)} %copy-done.4, f32[768]{0:T(1024)S(1)} %copy-done.49, f32[768]{0:T(1024)S(1)} %copy-done.35, f32[384]{0:T(512)S(1)} %copy-done.41, f32[384]{0:T(512)S(1)} %copy-done.39), kind=kOutput, calls=%fused_computation.8 | convolution fusion | flops 1815773184 | bytes 8266752 | tf_op jit(solution)/shard_map/dot_general | solution.py:22
  195.9 2.9 convolution_convert_fusion.2
  198.8 6.1 %reshape.346 = bf16[8,192,4,192]{3,2,1,0:T(4,128)(2,1)S(1)} reshape(bf16[1536,768]{1,0:T(8,128)(2,1)} %convolution_convert_fusion.2) | data formatting | bytes 4718592 | tf_op jit(solution)/shard_map/reshape | solution.py:419
  207.1 4.6 reshape.347
  213.5 3.5 stack.77
  217.3 4.4 stack.76
  223.4 4.6 stack.75
  232.4 6.4 %reshape.348 = bf16[32,144,384]{2,1,0:T(8,128)(2,1)S(1)} reshape(bf16[8,4,3,96,192]{4,3,2,1,0:T(8,128)(2,1)} %maximum_bitcast_fusion) | data formatting | bytes 7077888 | tf_op jit(solution)/shard_map/reshape | solution.py:422
  238.8 4.4 reshape.349
  243.2 2.8 copy.77
  246.1 3.6 reshape.350
  249.7 9.7 %reshape.351 = bf16[8,96,4,768]{3,2,1,0:T(4,128)(2,1)} reshape(bf16[768,3072]{1,0:T(8,128)(2,1)} %convolution_convert_fusion.1) | data formatting | bytes 9437184 | tf_op jit(solution)/shard_map/reshape | solution.py:419
  259.4 5.3 %copy.75 = bf16[8,96,4,768]{3,1,2,0:T(8,128)(2,1)} copy(bf16[8,96,4,768]{3,2,1,0:T(4,128)(2,1)} %reshape.351) | data formatting | bytes 9437184 | tf_op jit(solution)/shard_map/reshape | solution.py:419
  264.8 8.1 %reshape.352 = bf16[32,192,384]{2,1,0:T(8,128)(2,1)} reshape(bf16[8,4,96,768]{3,2,1,0:T(8,128)(2,1)} %bitcast.144) | data formatting | bytes 9437184 | tf_op jit(solution)/shard_map/reshape | solution.py:422
  272.8 6.7 %convolution_convert_fusion = bf16[768,3072]{1,0:T(8,128)(2,1)} fusion(bf16[384,3072]{1,0:T(8,128)(2,1)} %get-tuple-element.98, bf16[384,768]{1,0:T(8,128)(2,1)} %param.37, bf16[384]{0:T(512)(128)(2,1)} %copy-done.51), kind=kOutput, calls=%fused_computation.7 | convolution fusion | flops 1814593536 | bytes 7668480 | tf_op jit(solution)/shard_map/dot_general | solution.py:22
  279.5 9.7 %reshape.353 = bf16[8,96,4,768]{3,2,1,0:T(4,128)(2,1)} reshape(bf16[768,3072]{1,0:T(8,128)(2,1)} %convolution_convert_fusion) | data formatting | bytes 9437184 | tf_op jit(solution)/shard_map/reshape | solution.py:419
  289.3 5.3 %copy.74 = bf16[8,96,4,768]{3,1,2,0:T(8,128)(2,1)} copy(bf16[8,96,4,768]{3,2,1,0:T(4,128)(2,1)} %reshape.353) | data formatting | bytes 9437184 | tf_op jit(solution)/shard_map/reshape | solution.py:419
  294.6 8.3 %reshape.354 = bf16[32,192,384]{2,1,0:T(8,128)(2,1)} reshape(bf16[8,4,96,768]{3,2,1,0:T(8,128)(2,1)} %bitcast.145) | data formatting | bytes 9437184 | tf_op jit(solution)/shard_map/reshape | solution.py:422
  306.2 5.4 %constant_dynamic-update-slice_fusion.8 = bf16[32,672,384]{2,1,0:T(8,128)(2,1)} fusion(bf16[32,672,384]{2,1,0:T(8,128)(2,1)} %constant_dynamic-update-slice_fusion.9, bf16[32,192,384]{2,1,0:T(8,128)(2,1)} %reshape.352), kind=kLoop, calls=%fused_computation.109 | loop fusion | bytes 9437184
  315.9 42.0 %psum.7 = f32[4,13,192]{2,1,0:T(8,128)S(1)} all-reduce(f32[4,13,192]{2,1,0:T(8,128)S(1)} %pad_maximum_fusion), channel_id=1, replica_groups=mesh['dp'=8,'mp'=4] {'dp','mp'}, use_global_device_ids=true, to_apply=%region_22.23 | all-reduce | flops 9984 | bytes 79872 | tf_op jit(solution)/shard_map/psum | solution.py:435
  363.2 5.2 fusion.18
  368.4 137.7 %reduce-scatter.2.cloned.1.call-done = bf16[1,672,384]{2,1,0:T(8,128)(2,1)} async-done(((bf16[32,672,384]{2,1,0:T(8,128)(2,1)}), bf16[1,672,384]{2,1,0:T(8,128)(2,1)}) %reduce-scatter.2.cloned.1.call-update) | async-done | bytes 516112 | tf_op jit(solution)/shard_map/reduce_scatter | solution.py:423
  (232 shorter events, 71.6 us)
Async XLA Ops:
  7.2 95.7 %copy-start.15 = (bf16[384,768]{1,0:T(8,128)(2,1)S(1)}, bf16[384,768]{1,0:T(8,128)(2,1)}, u32[]{:S(2)}) copy-start(bf16[384,768]{1,0:T(8,128)(2,1)} %param.19) | copy-start | bytes 1769476
  7.2 498.8 %reduce-scatter.2.cloned.1.call-start = ((), (), s32[]{:S(2)}) async-start(), calls=%async_computation.1 | async-start | bytes 17031168 | tf_op jit(solution)/shard_map/reduce_scatter | solution.py:423
  7.8 96.0 %copy-start.16 = (bf16[384,768]{1,0:T(8,128)(2,1)S(1)}, bf16[384,768]{1,0:T(8,128)(2,1)}, u32[]{:S(2)}) copy-start(bf16[384,768]{1,0:T(8,128)(2,1)} %param.20) | copy-start | bytes 1769476
  103.1 4.1 copy-start.23
  103.8 3.4 copy-start.21
  103.8 3.7 copy-start.13
  109.0 3.5 copy-start.31
  109.9 15.4 %copy-start.17 = (bf16[384,768]{0,1:T(8,128)(2,1)}, bf16[384,768]{0,1:T(8,128)(2,1)S(1)}, u32[]{:S(2)}) copy-start(bf16[384,768]{0,1:T(8,128)(2,1)S(1)} %copy.50) | copy-start | bytes 1769476
  116.2 9.1 %copy-start.7 = (bf16[384,768]{0,1:T(8,128)(2,1)}, bf16[384,768]{0,1:T(8,128)(2,1)S(1)}, u32[]{:S(2)}) copy-start(bf16[384,768]{0,1:T(8,128)(2,1)S(1)} %copy.52) | copy-start | bytes 1769476
  117.8 12.3 %copy-start.48 = (f32[768]{0:T(1024)}, f32[768]{0:T(1024)S(1)}, u32[]{:S(2)}) copy-start(f32[768]{0:T(1024)S(1)} %add.152) | copy-start | bytes 9220
  118.5 27.0 %copy-start.34 = (f32[768]{0:T(1024)}, f32[768]{0:T(1024)S(1)}, u32[]{:S(2)}) copy-start(f32[768]{0:T(1024)S(1)} %mul.210) | copy-start | bytes 9220
  119.2 17.4 %copy-start.51 = (bf16[384]{0:T(512)(128)(2,1)}, bf16[384]{0:T(512)(128)(2,1)S(1)}, u32[]{:S(2)}) copy-start(bf16[384]{0:T(512)(128)(2,1)S(1)} %convert_element_type.159) | copy-start | bytes 2308
  125.3 3.8 copy-start.6
  125.3 3.8 copy-start.33
  129.1 7.5 %slice-start.2 = ((s8[4718592]{0:T(1024)(128)(4,1)}), s8[4194304]{0:T(1024)(128)(4,1)S(1)}, s32[]{:S(2)}) async-start(s8[4718592]{0:T(1024)(128)(4,1)} %bitcast.193), calls=%async_computation.4 | async-start | bytes 8388608
  129.1 13.5 %slice-start.4 = ((s8[4718592]{0:T(1024)(128)(4,1)}), s8[4194304]{0:T(1024)(128)(4,1)S(1)}, s32[]{:S(2)}) async-start(s8[4718592]{0:T(1024)(128)(4,1)} %bitcast.195), calls=%async_computation.6 | async-start | bytes 8388608
  130.0 15.5 %copy-start.3 = (f32[384,768]{1,0:T(8,128)}, f32[384,768]{1,0:T(8,128)S(1)}, u32[]{:S(2)}) copy-start(f32[384,768]{1,0:T(8,128)S(1)} %get-tuple-element.97) | copy-start | bytes 3538948
  130.1 15.4 %copy-start.38 = (f32[384]{0:T(512)}, f32[384]{0:T(512)S(1)}, u32[]{:S(2)}) copy-start(f32[384]{0:T(512)S(1)} %get-tuple-element.90) | copy-start | bytes 4612
  130.1 15.4 %copy-start.40 = (f32[384]{0:T(512)}, f32[384]{0:T(512)S(1)}, u32[]{:S(2)}) copy-start(f32[384]{0:T(512)S(1)} %get-tuple-element.91) | copy-start | bytes 4612
  130.1 6.5 %copy-start.19 = (bf16[384,768]{1,0:T(8,128)(2,1)S(1)}, bf16[384,768]{1,0:T(8,128)(2,1)}, u32[]{:S(2)}) copy-start(bf16[384,768]{1,0:T(8,128)(2,1)} %param.37) | copy-start | bytes 1769476
  130.1 6.5 %slice-start.3 = ((s8[4718592]{0:T(1024)(128)(4,1)}), s8[524288]{0:T(1024)(128)(4,1)S(1)}, s32[]{:S(2)}) async-start(s8[4718592]{0:T(1024)(128)(4,1)} %bitcast.193), calls=%async_computation.5 | async-start | bytes 1048576
  130.1 12.5 %slice-start.5 = ((s8[4718592]{0:T(1024)(128)(4,1)}), s8[524288]{0:T(1024)(128)(4,1)S(1)}, s32[]{:S(2)}) async-start(s8[4718592]{0:T(1024)(128)(4,1)} %bitcast.195), calls=%async_computation.7 | async-start | bytes 1048576
  149.7 7.5 %copy-start.25 = (f32[12,384]{1,0:T(8,128)S(1)}, f32[12,384]{1,0:T(8,128)}, u32[]{:S(2)}) copy-start(f32[12,384]{1,0:T(8,128)} %get-tuple-element.95) | copy-start | bytes 55300
  157.2 6.3 %copy-start.8 = (bf16[384,768]{0,1:T(8,128)(2,1)S(1)}, bf16[384,768]{0,1:T(8,128)(2,1)}, u32[]{:S(2)}) copy-start(bf16[384,768]{0,1:T(8,128)(2,1)} %copy-done.7) | copy-start | bytes 1769476
  165.7 5.2 %copy-start.14 = (bf16[3,768,768]{2,1,0:T(8,128)(2,1)S(1)}, bf16[3,768,768]{2,1,0:T(8,128)(2,1)}, u32[]{:S(2)}) copy-start(bf16[3,768,768]{2,1,0:T(8,128)(2,1)} %get-tuple-element.25) | copy-start | bytes 10616836
  171.6 3.8 copy-start.58
  305.0 6.6 %slice-start = ((s8[4718592]{0:T(1024)(128)(4,1)}), s8[4194304]{0:T(1024)(128)(4,1)S(1)}, s32[]{:S(2)}) async-start(s8[4718592]{0:T(1024)(128)(4,1)} %bitcast.142), calls=%async_computation.2 | async-start | bytes 8388608
  306.2 5.4 %slice-start.1 = ((s8[4718592]{0:T(1024)(128)(4,1)}), s8[524288]{0:T(1024)(128)(4,1)S(1)}, s32[]{:S(2)}) async-start(s8[4718592]{0:T(1024)(128)(4,1)} %bitcast.142), calls=%async_computation.3 | async-start | bytes 1048576
  314.3 45.5 %copy-start.1 = (bf16[384,768]{1,0:T(8,128)(2,1)S(1)}, bf16[384,768]{1,0:T(8,128)(2,1)}, u32[]{:S(2)}) copy-start(bf16[384,768]{1,0:T(8,128)(2,1)} %copy-done) | copy-start | bytes 1769476
  314.3 45.5 %copy-start.9 = (bf16[1536,768]{1,0:T(8,128)(2,1)S(1)}, bf16[1536,768]{1,0:T(8,128)(2,1)}, u32[]{:S(2)}) copy-start(bf16[1536,768]{1,0:T(8,128)(2,1)} %get-tuple-element.23) | copy-start | bytes 7077892
  359.8 3.4 copy-start.56
  506.0 3.5 copy-start.12
  (34 other events, 53.8 us)
Sparse Core Ops, SparseCore 0:
  314.5 191.5 reduce-scatter.1
